TPU v7x, 256 devices: a whole 4x4x8 slice. The times are simulated.
256 devices in a mesh: batch: 16 (over x_lo, z), seq: 16 (over x_hi, y, core).
Axes of the slice: x: 4 (x_hi: 2, x_lo: 2; x = x_hi * 2 + x_lo), y: 4, z: 8, core: 2. Of those that a mesh axis runs over, the one named last changes fastest.
Arguments:
- hidden_in: bfloat16 [16, 2048, 2048], P('batch', 'seq'), may hold values from -6 to 6
- queries: bfloat16 [16, 2048, 2048], P('batch', 'seq'), may hold values from -5 to 5
- key_states: bfloat16 [16, 2048, 512], P('batch', 'seq'), may hold values from -12 to 12
- value_states: bfloat16 [16, 2048, 512], P('batch', 'seq'), may hold values from -6 to 6
- grad_out: bfloat16 [16, 2048, 2048], P('batch', 'seq'), may hold values from -6 to 6
- log_sums: float32 [16, 16, 2048], P('batch', None, 'seq'), may hold values from -700 to 700, as said below
- deltas: float32 [16, 16, 2048], P('batch', None, 'seq'), may hold values from -6 to 6
- block_order: int32 [32], replicated, may hold values from 0 to 31, as said below
Outputs:
- grad_queries: bfloat16 [16, 2048, 2048], P('batch', 'seq')
- grad_keys: bfloat16 [16, 2048, 512], P('batch', 'seq')
- grad_values: bfloat16 [16, 2048, 512], P('batch', 'seq')
- key_wgrad: float32 [2048, 512], P(('batch', 'seq'))
- value_wgrad: float32 [2048, 512], P(('batch', 'seq'))
Inputs may be any that keep to these rules, and one draw needn't show every extreme that they name: `block_order`: entries 2i and 2i+1 name blocks c and 31 - c for some c, in either order; the 32 entries together are a permutation of 0 to 31. `log_sums`: each entry lies within 0.1 of the log of the sum over visible j of exp(scores[b,h,i,j]).
All inputs are finite; a program needn't handle non-finite values.
Results may differ from a plain program's by a relative error of at most 0.0049.
Values may be sent and summed in bfloat16 or wider, within the bound.
A program may use at most 64 MiB of HBM per device.

v0:
```python
import math

import jax
import jax.numpy as jnp
from jax import lax
from jax.sharding import PartitionSpec as P

HQ = 16
HK = 4
DH = 128


MASKED = -1e30


def passed_along(value, axis, steps):
    count = lax.axis_size(axis)
    pairs = [(source, (source + steps) % count) for source in range(count)]
    return lax.ppermute(value, axis, pairs)


def in_blocks(shard, dim, count):
    shape = shard.shape
    parts = shard.reshape(*shape[:dim], count, shape[dim] // count, *shape[dim + 1 :])
    return jnp.moveaxis(parts, dim, 0)


def summed_on_arrival(shard, axis, dim):
    parts = in_blocks(shard, dim, lax.axis_size(axis))
    arrived = lax.all_to_all(parts, axis, split_axis=0, concat_axis=0, tiled=True)
    return arrived.sum(axis=0)


def stored_positions(block_order, first_row, row_count, span_rows):
    row_ids = first_row + jnp.arange(row_count, dtype=jnp.int32)
    slot_ids = row_ids // span_rows
    matches = slot_ids[:, None] == jnp.arange(block_order.shape[0], dtype=jnp.int32)[None, :]
    block_ids = jnp.sum(jnp.where(matches, block_order[None, :], 0), axis=1)
    return block_ids * span_rows + row_ids % span_rows


def head_scores(left_heads, right_block):
    batch_rows, right_rows = (right_block.shape[0], right_block.shape[1])
    right_heads = right_block.reshape(batch_rows, right_rows, HK, DH)
    return jnp.einsum(
        "bqhgd,bkhd->bhgqk", left_heads, right_heads, preferred_element_type=jnp.float32
    )


def masked_scores(query_heads, key_block, query_pos, key_pos):
    scores = head_scores(query_heads, key_block) * (1.0 / math.sqrt(DH))
    visible = key_pos[None, :] <= query_pos[:, None]
    return jnp.where(visible, scores, MASKED)


def grad_block(
    query_heads, grad_heads, query_pos, row_lse, row_deltas, key_block, value_block, key_pos
):
    scores = masked_scores(query_heads, key_block, query_pos, key_pos)
    probs = jnp.exp(scores - row_lse[..., None])
    grad_probs = head_scores(grad_heads, value_block)
    grad_scores = (probs * (grad_probs - row_deltas[..., None]) * (1.0 / math.sqrt(DH))).astype(
        jnp.bfloat16
    )
    probs_low = probs.astype(jnp.bfloat16)
    batch_rows, key_rows = (key_block.shape[0], key_block.shape[1])
    key_heads = key_block.reshape(batch_rows, key_rows, HK, DH)
    query_part = jnp.einsum(
        "bhgqk,bkhd->bqhgd", grad_scores, key_heads, preferred_element_type=jnp.float32
    )
    key_part = jnp.einsum(
        "bhgqk,bqhgd->bkhd", grad_scores, query_heads, preferred_element_type=jnp.float32
    )
    value_part = jnp.einsum(
        "bhgqk,bqhgd->bkhd", probs_low, grad_heads, preferred_element_type=jnp.float32
    )
    key_part = key_part.reshape(batch_rows, key_rows, HK * DH)
    value_part = value_part.reshape(batch_rows, key_rows, HK * DH)
    return (query_part, key_part, value_part)


def shards(hidden_in, queries, key_states, value_states, grad_out, log_sums, deltas, block_order):
    seq_count = lax.axis_size("seq")
    my_index = lax.axis_index("seq")
    batch_rows, local_rows = (queries.shape[0], queries.shape[1])
    span_rows = local_rows // 2
    group_size = HQ // HK
    query_heads = queries.reshape(batch_rows, local_rows, HK, group_size, DH)
    grad_heads = grad_out.reshape(batch_rows, local_rows, HK, group_size, DH)
    row_lse = log_sums.reshape(batch_rows, HK, group_size, local_rows)
    row_deltas = deltas.reshape(batch_rows, HK, group_size, local_rows)
    query_pos = stored_positions(block_order, my_index * local_rows, local_rows, span_rows)
    key_zeros = jnp.zeros(key_states.shape, jnp.float32)
    query_zeros = jnp.zeros(query_heads.shape, jnp.float32)

    def block_grads(accums, key_block, value_block, source):
        key_acc, value_acc, query_acc = accums
        key_pos = stored_positions(block_order, source * local_rows, local_rows, span_rows)
        query_part, key_part, value_part = grad_block(
            query_heads, grad_heads, query_pos, row_lse, row_deltas, key_block, value_block, key_pos
        )
        return (key_acc + key_part, value_acc + value_part, query_acc + query_part)

    def one_turn(turn_index, turn_state):
        key_block, value_block = (turn_state[0], turn_state[1])
        source = (my_index - turn_index) % seq_count
        key_acc, value_acc, query_acc = block_grads(turn_state[2:], key_block, value_block, source)
        key_acc, value_acc = passed_along((key_acc, value_acc), "seq", 1)
        return (key_block, value_block, key_acc, value_acc, query_acc)

    def loop_turn(turn_index, turn_state):
        turn_state = one_turn(turn_index, turn_state)
        key_block, value_block = passed_along((turn_state[0], turn_state[1]), "seq", 1)
        return (key_block, value_block) + tuple(turn_state[2:])

    turn_state = lax.fori_loop(
        0, seq_count - 1, loop_turn, (key_states, value_states, key_zeros, key_zeros, query_zeros)
    )
    turn_state = one_turn(seq_count - 1, turn_state)
    key_acc, value_acc, query_acc = (turn_state[2], turn_state[3], turn_state[4])
    grad_keys = key_acc.astype(jnp.bfloat16)
    grad_values = value_acc.astype(jnp.bfloat16)
    grad_queries = query_acc.reshape(batch_rows, local_rows, HQ * DH).astype(jnp.bfloat16)
    key_width = HK * DH
    token_grads = jnp.concatenate([grad_keys, grad_values], axis=2).reshape(
        batch_rows * local_rows, 2 * key_width
    )
    flat_hidden = hidden_in.reshape(batch_rows * local_rows, hidden_in.shape[2])
    batch_sums = lax.psum_scatter(
        jnp.einsum("td,te->de", flat_hidden, token_grads, preferred_element_type=jnp.float32),
        "batch",
        scatter_dimension=0,
        tiled=True,
    )
    weight_grads = summed_on_arrival(batch_sums, "seq", 0)
    return (
        grad_queries,
        grad_keys,
        grad_values,
        weight_grads[:, :key_width],
        weight_grads[:, key_width:],
    )


def solution(mesh):
    in_specs = (
        P("batch", "seq", None),
        P("batch", "seq", None),
        P("batch", "seq", None),
        P("batch", "seq", None),
        P("batch", "seq", None),
        P("batch", None, "seq"),
        P("batch", None, "seq"),
        P(),
    )
    out_specs = (
        P("batch", "seq", None),
        P("batch", "seq", None),
        P("batch", "seq", None),
        P(("batch", "seq"), None),
        P(("batch", "seq"), None),
    )
    return jax.shard_map(shards, mesh=mesh, in_specs=in_specs, out_specs=out_specs, check_vma=False)
```

profile of v0, /device:TPU:2, one launch (start us, length us, event | category | flops | bytes accessed | tf_op | source)
XLA Modules:
  0.0 486.1 jit_solution(5020239510545587013)
XLA Ops:
  15.2 316.1 %while.25 = (s32[]{:T(128)}, bf16[1,128,512]{2,1,0:T(8,128)(2,1)}, bf16[1,128,512]{2,1,0:T(8,128)(2,1)}, f32[1,128,512]{1,2,0:T(8,128)}, f32[1,128,512]{1,2,0:T(...) while((s32[]{:T(128)}, bf16[1,128,512]{2,1,0:T(8,128)(2,1)}, ...), condition=%wide.region_3.4_spmd.clone, body=%wide.region_1.3_spmd.clone.sunk | while | flops 338329216 | bytes 15650908 | solution.py:116
  17.7 1.7 collective-permute-start.1
  23.6 1.7 add.356
  25.7 1.7 add.357
  29.5 5.5 %collective-permute-done.2 = f32[1,128,512]{1,2,0:T(8,128)} collective-permute-done((f32[1,128,512]{1,2,0:T(8,128)}, f32[1,128,512]{1,2,0:T(8,128)}, u32[]{:S(2)}, u32[]{:S(2)}) %collective-permute-start.2) | collective-permute-done | bytes 262176 | tf_op jit(solution)/shard_map/while/body/eval_jaxpr/ppermute | solution.py:19
  35.1 2.8 collective-permute-done.3
  44.6 1.7 add.356
  46.6 1.7 add.357
  48.8 7.2 %collective-permute-done.2 = f32[1,128,512]{1,2,0:T(8,128)} collective-permute-done((f32[1,128,512]{1,2,0:T(8,128)}, f32[1,128,512]{1,2,0:T(8,128)}, u32[]{:S(2)}, u32[]{:S(2)}) %collective-permute-start.2) | collective-permute-done | bytes 262176 | tf_op jit(solution)/shard_map/while/body/eval_jaxpr/ppermute | solution.py:19
  56.0 2.8 collective-permute-done.3
  65.5 1.7 add.356
  67.5 1.7 add.357
  69.7 7.2 %collective-permute-done.2 = f32[1,128,512]{1,2,0:T(8,128)} collective-permute-done((f32[1,128,512]{1,2,0:T(8,128)}, f32[1,128,512]{1,2,0:T(8,128)}, u32[]{:S(2)}, u32[]{:S(2)}) %collective-permute-start.2) | collective-permute-done | bytes 262176 | tf_op jit(solution)/shard_map/while/body/eval_jaxpr/ppermute | solution.py:19
  77.0 2.8 collective-permute-done.3
  86.5 1.7 add.356
  88.5 1.7 add.357
  90.7 7.2 %collective-permute-done.2 = f32[1,128,512]{1,2,0:T(8,128)} collective-permute-done((f32[1,128,512]{1,2,0:T(8,128)}, f32[1,128,512]{1,2,0:T(8,128)}, u32[]{:S(2)}, u32[]{:S(2)}) %collective-permute-start.2) | collective-permute-done | bytes 262176 | tf_op jit(solution)/shard_map/while/body/eval_jaxpr/ppermute | solution.py:19
  97.9 2.8 collective-permute-done.3
  107.4 1.7 add.356
  109.4 1.7 add.357
  111.7 7.2 %collective-permute-done.2 = f32[1,128,512]{1,2,0:T(8,128)} collective-permute-done((f32[1,128,512]{1,2,0:T(8,128)}, f32[1,128,512]{1,2,0:T(8,128)}, u32[]{:S(2)}, u32[]{:S(2)}) %collective-permute-start.2) | collective-permute-done | bytes 262176 | tf_op jit(solution)/shard_map/while/body/eval_jaxpr/ppermute | solution.py:19
  118.9 2.8 collective-permute-done.3
  128.4 1.7 add.356
  130.4 1.7 add.357
  132.6 7.2 %collective-permute-done.2 = f32[1,128,512]{1,2,0:T(8,128)} collective-permute-done((f32[1,128,512]{1,2,0:T(8,128)}, f32[1,128,512]{1,2,0:T(8,128)}, u32[]{:S(2)}, u32[]{:S(2)}) %collective-permute-start.2) | collective-permute-done | bytes 262176 | tf_op jit(solution)/shard_map/while/body/eval_jaxpr/ppermute | solution.py:19
  139.9 2.8 collective-permute-done.3
  149.4 1.7 add.356
  151.4 1.7 add.357
  153.6 7.2 %collective-permute-done.2 = f32[1,128,512]{1,2,0:T(8,128)} collective-permute-done((f32[1,128,512]{1,2,0:T(8,128)}, f32[1,128,512]{1,2,0:T(8,128)}, u32[]{:S(2)}, u32[]{:S(2)}) %collective-permute-start.2) | collective-permute-done | bytes 262176 | tf_op jit(solution)/shard_map/while/body/eval_jaxpr/ppermute | solution.py:19
  160.8 2.8 collective-permute-done.3
  170.3 1.7 add.356
  172.3 1.7 add.357
  174.5 7.2 %collective-permute-done.2 = f32[1,128,512]{1,2,0:T(8,128)} collective-permute-done((f32[1,128,512]{1,2,0:T(8,128)}, f32[1,128,512]{1,2,0:T(8,128)}, u32[]{:S(2)}, u32[]{:S(2)}) %collective-permute-start.2) | collective-permute-done | bytes 262176 | tf_op jit(solution)/shard_map/while/body/eval_jaxpr/ppermute | solution.py:19
  181.8 2.8 collective-permute-done.3
  191.3 1.7 add.356
  193.3 1.7 add.357
  195.5 7.2 %collective-permute-done.2 = f32[1,128,512]{1,2,0:T(8,128)} collective-permute-done((f32[1,128,512]{1,2,0:T(8,128)}, f32[1,128,512]{1,2,0:T(8,128)}, u32[]{:S(2)}, u32[]{:S(2)}) %collective-permute-start.2) | collective-permute-done | bytes 262176 | tf_op jit(solution)/shard_map/while/body/eval_jaxpr/ppermute | solution.py:19
  202.7 2.8 collective-permute-done.3
  212.2 1.7 add.356
  216.5 7.2 %collective-permute-done.2 = f32[1,128,512]{1,2,0:T(8,128)} collective-permute-done((f32[1,128,512]{1,2,0:T(8,128)}, f32[1,128,512]{1,2,0:T(8,128)}, u32[]{:S(2)}, u32[]{:S(2)}) %collective-permute-start.2) | collective-permute-done | bytes 262176 | tf_op jit(solution)/shard_map/while/body/eval_jaxpr/ppermute | solution.py:19
  223.7 2.8 collective-permute-done.3
  233.2 1.7 add.356
  237.4 7.2 %collective-permute-done.2 = f32[1,128,512]{1,2,0:T(8,128)} collective-permute-done((f32[1,128,512]{1,2,0:T(8,128)}, f32[1,128,512]{1,2,0:T(8,128)}, u32[]{:S(2)}, u32[]{:S(2)}) %collective-permute-start.2) | collective-permute-done | bytes 262176 | tf_op jit(solution)/shard_map/while/body/eval_jaxpr/ppermute | solution.py:19
  244.7 2.8 collective-permute-done.3
  254.2 1.7 add.356
  258.4 7.2 %collective-permute-done.2 = f32[1,128,512]{1,2,0:T(8,128)} collective-permute-done((f32[1,128,512]{1,2,0:T(8,128)}, f32[1,128,512]{1,2,0:T(8,128)}, u32[]{:S(2)}, u32[]{:S(2)}) %collective-permute-start.2) | collective-permute-done | bytes 262176 | tf_op jit(solution)/shard_map/while/body/eval_jaxpr/ppermute | solution.py:19
  265.6 2.8 collective-permute-done.3
  275.1 1.7 add.356
  279.3 7.2 %collective-permute-done.2 = f32[1,128,512]{1,2,0:T(8,128)} collective-permute-done((f32[1,128,512]{1,2,0:T(8,128)}, f32[1,128,512]{1,2,0:T(8,128)}, u32[]{:S(2)}, u32[]{:S(2)}) %collective-permute-start.2) | collective-permute-done | bytes 262176 | tf_op jit(solution)/shard_map/while/body/eval_jaxpr/ppermute | solution.py:19
  286.6 2.8 collective-permute-done.3
  296.1 1.7 add.356
  300.3 7.2 %collective-permute-done.2 = f32[1,128,512]{1,2,0:T(8,128)} collective-permute-done((f32[1,128,512]{1,2,0:T(8,128)}, f32[1,128,512]{1,2,0:T(8,128)}, u32[]{:S(2)}, u32[]{:S(2)}) %collective-permute-start.2) | collective-permute-done | bytes 262176 | tf_op jit(solution)/shard_map/while/body/eval_jaxpr/ppermute | solution.py:19
  307.5 2.8 collective-permute-done.3
  317.0 1.7 add.356
  321.3 7.2 %collective-permute-done.2 = f32[1,128,512]{1,2,0:T(8,128)} collective-permute-done((f32[1,128,512]{1,2,0:T(8,128)}, f32[1,128,512]{1,2,0:T(8,128)}, u32[]{:S(2)}, u32[]{:S(2)}) %collective-permute-start.2) | collective-permute-done | bytes 262176 | tf_op jit(solution)/shard_map/while/body/eval_jaxpr/ppermute | solution.py:19
  328.5 2.8 collective-permute-done.3
  333.4 1.8 copy.85
  342.3 5.3 %collective-permute-done.4 = bf16[1,128,512]{2,1,0:T(8,128)(2,1)S(1)} collective-permute-done((bf16[1,128,512]{2,1,0:T(8,128)(2,1)}, bf16[1,128,512]{2,1,0:T(8,128)(2,1)S(1)}, u32[]{:S(2)}, u32[]{:S(2)}) %collective-permute-start.4) | collective-permute-done | bytes 131104 | tf_op jit(solution)/shard_map/ppermute | solution.py:19
  347.7 2.7 collective-permute-done.5
  350.4 4.5 convolution_bitcast_fusion.2
  354.9 100.7 %reduce-scatter.2.cloned.1.call-done = f32[128,1024]{0,1:T(8,128)} async-done(((f32[2048,1024]{0,1:T(8,128)}), f32[128,1024]{0,1:T(8,128)}) %reduce-scatter.2.cloned.1.call-update) | async-done | bytes 524304 | tf_op jit(solution)/shard_map/reduce_scatter | solution.py:129
  455.6 2.0 copy.91
  457.6 6.2 %all-to-all-start = ((f32[16,8,1024]{2,1,0:T(8,128)}), f32[16,8,1024]{2,1,0:T(8,128)}, u32[]{:S(2)}, u32[]{:S(2)}) async-start(f32[16,8,1024]{2,1,0:T(8,128)} %bitcast.31), calls=%async_computation.1 | async-start | bytes 1048576 | tf_op jit(solution)/shard_map/all_to_all | solution.py:30
  465.5 10.7 %all-to-all-done = f32[16,8,1024]{2,1,0:T(8,128)} async-done(((f32[16,8,1024]{2,1,0:T(8,128)}), f32[16,8,1024]{2,1,0:T(8,128)}, u32[]{:S(2)}, u32[]{:S(2)}) %all-to-all-start) | async-done | bytes 524320 | tf_op jit(solution)/shard_map/all_to_all | solution.py:30
  (329 shorter events, 145.1 us)
Async XLA Ops:
  7.2 448.4 %reduce-scatter.2.cloned.1.call-start = ((), (), s32[]{:S(2)}) async-start(), calls=%async_computation.2 | async-start | bytes 8912896 | tf_op jit(solution)/shard_map/reduce_scatter | solution.py:129
  16.2 13.4 %collective-permute-start = (bf16[1,128,512]{2,1,0:T(8,128)(2,1)S(1)}, bf16[1,128,512]{2,1,0:T(8,128)(2,1)}, u32[]{:S(2)}, u32[]{:S(2)}) collective-permute-start(bf16[1,128,512]{2,1,0:T(8,128)(2,1)S(1)} %copy.146), channel_id=1, source_target_pairs={{0,1},{1,2},{2,3},{3,4},{4,5},{5,6},{6,7},{7,8},{8,9},{9,10},{10,1... | collective-permute-start | bytes 393224 | tf_op jit(solution)/shard_map/while/body/eval_jaxpr/ppermute | solution.py:19
  17.7 11.8 %collective-permute-start.1 = (bf16[1,128,512]{2,1,0:T(8,128)(2,1)}, bf16[1,128,512]{2,1,0:T(8,128)(2,1)}, u32[]{:S(2)}, u32[]{:S(2)}) collective-permute-start(bf16[1,128,512]{2,1,0:T(8,128)(2,1)} %copy.147), channel_id=1, source_target_pairs={{0,1},{1,2},{2,3},{3,4},{4,5},{5,6},{6,7},{7,8},{8,9},{9,10},{10,1... | collective-permute-start | bytes 393224 | tf_op jit(solution)/shard_map/while/body/eval_jaxpr/ppermute | solution.py:19
  25.3 9.7 %collective-permute-start.2 = (f32[1,128,512]{1,2,0:T(8,128)}, f32[1,128,512]{1,2,0:T(8,128)}, u32[]{:S(2)}, u32[]{:S(2)}) collective-permute-start(f32[1,128,512]{1,2,0:T(8,128)} %add.356), channel_id=1, source_target_pairs={{0,1},{1,2},{2,3},{3,4},{4,5},{5,6},{6,7},{7,8},{8,9},{9,10},{10,1... | collective-permute-start | bytes 786440 | tf_op jit(solution)/shard_map/while/body/eval_jaxpr/ppermute | solution.py:19
  27.4 10.5 %collective-permute-start.3 = (f32[1,128,512]{1,2,0:T(8,128)}, f32[1,128,512]{1,2,0:T(8,128)}, u32[]{:S(2)}, u32[]{:S(2)}) collective-permute-start(f32[1,128,512]{1,2,0:T(8,128)} %add.357), channel_id=1, source_target_pairs={{0,1},{1,2},{2,3},{3,4},{4,5},{5,6},{6,7},{7,8},{8,9},{9,10},{10,1... | collective-permute-start | bytes 786440 | tf_op jit(solution)/shard_map/while/body/eval_jaxpr/ppermute | solution.py:19
  38.8 10.0 %collective-permute-start = (bf16[1,128,512]{2,1,0:T(8,128)(2,1)S(1)}, bf16[1,128,512]{2,1,0:T(8,128)(2,1)}, u32[]{:S(2)}, u32[]{:S(2)}) collective-permute-start(bf16[1,128,512]{2,1,0:T(8,128)(2,1)S(1)} %copy.146), channel_id=1, source_target_pairs={{0,1},{1,2},{2,3},{3,4},{4,5},{5,6},{6,7},{7,8},{8,9},{9,10},{10,1... | collective-permute-start | bytes 393224 | tf_op jit(solution)/shard_map/while/body/eval_jaxpr/ppermute | solution.py:19
  40.3 8.4 %collective-permute-start.1 = (bf16[1,128,512]{2,1,0:T(8,128)(2,1)}, bf16[1,128,512]{2,1,0:T(8,128)(2,1)}, u32[]{:S(2)}, u32[]{:S(2)}) collective-permute-start(bf16[1,128,512]{2,1,0:T(8,128)(2,1)} %copy.147), channel_id=1, source_target_pairs={{0,1},{1,2},{2,3},{3,4},{4,5},{5,6},{6,7},{7,8},{8,9},{9,10},{10,1... | collective-permute-start | bytes 393224 | tf_op jit(solution)/shard_map/while/body/eval_jaxpr/ppermute | solution.py:19
  46.3 9.8 %collective-permute-start.2 = (f32[1,128,512]{1,2,0:T(8,128)}, f32[1,128,512]{1,2,0:T(8,128)}, u32[]{:S(2)}, u32[]{:S(2)}) collective-permute-start(f32[1,128,512]{1,2,0:T(8,128)} %add.356), channel_id=1, source_target_pairs={{0,1},{1,2},{2,3},{3,4},{4,5},{5,6},{6,7},{7,8},{8,9},{9,10},{10,1... | collective-permute-start | bytes 786440 | tf_op jit(solution)/shard_map/while/body/eval_jaxpr/ppermute | solution.py:19
  48.3 10.6 %collective-permute-start.3 = (f32[1,128,512]{1,2,0:T(8,128)}, f32[1,128,512]{1,2,0:T(8,128)}, u32[]{:S(2)}, u32[]{:S(2)}) collective-permute-start(f32[1,128,512]{1,2,0:T(8,128)} %add.357), channel_id=1, source_target_pairs={{0,1},{1,2},{2,3},{3,4},{4,5},{5,6},{6,7},{7,8},{8,9},{9,10},{10,1... | collective-permute-start | bytes 786440 | tf_op jit(solution)/shard_map/while/body/eval_jaxpr/ppermute | solution.py:19
  59.7 10.0 %collective-permute-start = (bf16[1,128,512]{2,1,0:T(8,128)(2,1)S(1)}, bf16[1,128,512]{2,1,0:T(8,128)(2,1)}, u32[]{:S(2)}, u32[]{:S(2)}) collective-permute-start(bf16[1,128,512]{2,1,0:T(8,128)(2,1)S(1)} %copy.146), channel_id=1, source_target_pairs={{0,1},{1,2},{2,3},{3,4},{4,5},{5,6},{6,7},{7,8},{8,9},{9,10},{10,1... | collective-permute-start | bytes 393224 | tf_op jit(solution)/shard_map/while/body/eval_jaxpr/ppermute | solution.py:19
  61.3 8.4 %collective-permute-start.1 = (bf16[1,128,512]{2,1,0:T(8,128)(2,1)}, bf16[1,128,512]{2,1,0:T(8,128)(2,1)}, u32[]{:S(2)}, u32[]{:S(2)}) collective-permute-start(bf16[1,128,512]{2,1,0:T(8,128)(2,1)} %copy.147), channel_id=1, source_target_pairs={{0,1},{1,2},{2,3},{3,4},{4,5},{5,6},{6,7},{7,8},{8,9},{9,10},{10,1... | collective-permute-start | bytes 393224 | tf_op jit(solution)/shard_map/while/body/eval_jaxpr/ppermute | solution.py:19
  67.2 9.8 %collective-permute-start.2 = (f32[1,128,512]{1,2,0:T(8,128)}, f32[1,128,512]{1,2,0:T(8,128)}, u32[]{:S(2)}, u32[]{:S(2)}) collective-permute-start(f32[1,128,512]{1,2,0:T(8,128)} %add.356), channel_id=1, source_target_pairs={{0,1},{1,2},{2,3},{3,4},{4,5},{5,6},{6,7},{7,8},{8,9},{9,10},{10,1... | collective-permute-start | bytes 786440 | tf_op jit(solution)/shard_map/while/body/eval_jaxpr/ppermute | solution.py:19
  69.2 10.6 %collective-permute-start.3 = (f32[1,128,512]{1,2,0:T(8,128)}, f32[1,128,512]{1,2,0:T(8,128)}, u32[]{:S(2)}, u32[]{:S(2)}) collective-permute-start(f32[1,128,512]{1,2,0:T(8,128)} %add.357), channel_id=1, source_target_pairs={{0,1},{1,2},{2,3},{3,4},{4,5},{5,6},{6,7},{7,8},{8,9},{9,10},{10,1... | collective-permute-start | bytes 786440 | tf_op jit(solution)/shard_map/while/body/eval_jaxpr/ppermute | solution.py:19
  80.7 10.0 %collective-permute-start = (bf16[1,128,512]{2,1,0:T(8,128)(2,1)S(1)}, bf16[1,128,512]{2,1,0:T(8,128)(2,1)}, u32[]{:S(2)}, u32[]{:S(2)}) collective-permute-start(bf16[1,128,512]{2,1,0:T(8,128)(2,1)S(1)} %copy.146), channel_id=1, source_target_pairs={{0,1},{1,2},{2,3},{3,4},{4,5},{5,6},{6,7},{7,8},{8,9},{9,10},{10,1... | collective-permute-start | bytes 393224 | tf_op jit(solution)/shard_map/while/body/eval_jaxpr/ppermute | solution.py:19
  82.3 8.4 %collective-permute-start.1 = (bf16[1,128,512]{2,1,0:T(8,128)(2,1)}, bf16[1,128,512]{2,1,0:T(8,128)(2,1)}, u32[]{:S(2)}, u32[]{:S(2)}) collective-permute-start(bf16[1,128,512]{2,1,0:T(8,128)(2,1)} %copy.147), channel_id=1, source_target_pairs={{0,1},{1,2},{2,3},{3,4},{4,5},{5,6},{6,7},{7,8},{8,9},{9,10},{10,1... | collective-permute-start | bytes 393224 | tf_op jit(solution)/shard_map/while/body/eval_jaxpr/ppermute | solution.py:19
  88.2 9.8 %collective-permute-start.2 = (f32[1,128,512]{1,2,0:T(8,128)}, f32[1,128,512]{1,2,0:T(8,128)}, u32[]{:S(2)}, u32[]{:S(2)}) collective-permute-start(f32[1,128,512]{1,2,0:T(8,128)} %add.356), channel_id=1, source_target_pairs={{0,1},{1,2},{2,3},{3,4},{4,5},{5,6},{6,7},{7,8},{8,9},{9,10},{10,1... | collective-permute-start | bytes 786440 | tf_op jit(solution)/shard_map/while/body/eval_jaxpr/ppermute | solution.py:19
  90.2 10.6 %collective-permute-start.3 = (f32[1,128,512]{1,2,0:T(8,128)}, f32[1,128,512]{1,2,0:T(8,128)}, u32[]{:S(2)}, u32[]{:S(2)}) collective-permute-start(f32[1,128,512]{1,2,0:T(8,128)} %add.357), channel_id=1, source_target_pairs={{0,1},{1,2},{2,3},{3,4},{4,5},{5,6},{6,7},{7,8},{8,9},{9,10},{10,1... | collective-permute-start | bytes 786440 | tf_op jit(solution)/shard_map/while/body/eval_jaxpr/ppermute | solution.py:19
  101.7 10.0 %collective-permute-start = (bf16[1,128,512]{2,1,0:T(8,128)(2,1)S(1)}, bf16[1,128,512]{2,1,0:T(8,128)(2,1)}, u32[]{:S(2)}, u32[]{:S(2)}) collective-permute-start(bf16[1,128,512]{2,1,0:T(8,128)(2,1)S(1)} %copy.146), channel_id=1, source_target_pairs={{0,1},{1,2},{2,3},{3,4},{4,5},{5,6},{6,7},{7,8},{8,9},{9,10},{10,1... | collective-permute-start | bytes 393224 | tf_op jit(solution)/shard_map/while/body/eval_jaxpr/ppermute | solution.py:19
  103.2 8.4 %collective-permute-start.1 = (bf16[1,128,512]{2,1,0:T(8,128)(2,1)}, bf16[1,128,512]{2,1,0:T(8,128)(2,1)}, u32[]{:S(2)}, u32[]{:S(2)}) collective-permute-start(bf16[1,128,512]{2,1,0:T(8,128)(2,1)} %copy.147), channel_id=1, source_target_pairs={{0,1},{1,2},{2,3},{3,4},{4,5},{5,6},{6,7},{7,8},{8,9},{9,10},{10,1... | collective-permute-start | bytes 393224 | tf_op jit(solution)/shard_map/while/body/eval_jaxpr/ppermute | solution.py:19
  109.1 9.8 %collective-permute-start.2 = (f32[1,128,512]{1,2,0:T(8,128)}, f32[1,128,512]{1,2,0:T(8,128)}, u32[]{:S(2)}, u32[]{:S(2)}) collective-permute-start(f32[1,128,512]{1,2,0:T(8,128)} %add.356), channel_id=1, source_target_pairs={{0,1},{1,2},{2,3},{3,4},{4,5},{5,6},{6,7},{7,8},{8,9},{9,10},{10,1... | collective-permute-start | bytes 786440 | tf_op jit(solution)/shard_map/while/body/eval_jaxpr/ppermute | solution.py:19
  111.1 10.6 %collective-permute-start.3 = (f32[1,128,512]{1,2,0:T(8,128)}, f32[1,128,512]{1,2,0:T(8,128)}, u32[]{:S(2)}, u32[]{:S(2)}) collective-permute-start(f32[1,128,512]{1,2,0:T(8,128)} %add.357), channel_id=1, source_target_pairs={{0,1},{1,2},{2,3},{3,4},{4,5},{5,6},{6,7},{7,8},{8,9},{9,10},{10,1... | collective-permute-start | bytes 786440 | tf_op jit(solution)/shard_map/while/body/eval_jaxpr/ppermute | solution.py:19
  122.6 10.0 %collective-permute-start = (bf16[1,128,512]{2,1,0:T(8,128)(2,1)S(1)}, bf16[1,128,512]{2,1,0:T(8,128)(2,1)}, u32[]{:S(2)}, u32[]{:S(2)}) collective-permute-start(bf16[1,128,512]{2,1,0:T(8,128)(2,1)S(1)} %copy.146), channel_id=1, source_target_pairs={{0,1},{1,2},{2,3},{3,4},{4,5},{5,6},{6,7},{7,8},{8,9},{9,10},{10,1... | collective-permute-start | bytes 393224 | tf_op jit(solution)/shard_map/while/body/eval_jaxpr/ppermute | solution.py:19
  124.2 8.4 %collective-permute-start.1 = (bf16[1,128,512]{2,1,0:T(8,128)(2,1)}, bf16[1,128,512]{2,1,0:T(8,128)(2,1)}, u32[]{:S(2)}, u32[]{:S(2)}) collective-permute-start(bf16[1,128,512]{2,1,0:T(8,128)(2,1)} %copy.147), channel_id=1, source_target_pairs={{0,1},{1,2},{2,3},{3,4},{4,5},{5,6},{6,7},{7,8},{8,9},{9,10},{10,1... | collective-permute-start | bytes 393224 | tf_op jit(solution)/shard_map/while/body/eval_jaxpr/ppermute | solution.py:19
  130.1 9.8 %collective-permute-start.2 = (f32[1,128,512]{1,2,0:T(8,128)}, f32[1,128,512]{1,2,0:T(8,128)}, u32[]{:S(2)}, u32[]{:S(2)}) collective-permute-start(f32[1,128,512]{1,2,0:T(8,128)} %add.356), channel_id=1, source_target_pairs={{0,1},{1,2},{2,3},{3,4},{4,5},{5,6},{6,7},{7,8},{8,9},{9,10},{10,1... | collective-permute-start | bytes 786440 | tf_op jit(solution)/shard_map/while/body/eval_jaxpr/ppermute | solution.py:19
  132.1 10.6 %collective-permute-start.3 = (f32[1,128,512]{1,2,0:T(8,128)}, f32[1,128,512]{1,2,0:T(8,128)}, u32[]{:S(2)}, u32[]{:S(2)}) collective-permute-start(f32[1,128,512]{1,2,0:T(8,128)} %add.357), channel_id=1, source_target_pairs={{0,1},{1,2},{2,3},{3,4},{4,5},{5,6},{6,7},{7,8},{8,9},{9,10},{10,1... | collective-permute-start | bytes 786440 | tf_op jit(solution)/shard_map/while/body/eval_jaxpr/ppermute | solution.py:19
  143.6 10.0 %collective-permute-start = (bf16[1,128,512]{2,1,0:T(8,128)(2,1)S(1)}, bf16[1,128,512]{2,1,0:T(8,128)(2,1)}, u32[]{:S(2)}, u32[]{:S(2)}) collective-permute-start(bf16[1,128,512]{2,1,0:T(8,128)(2,1)S(1)} %copy.146), channel_id=1, source_target_pairs={{0,1},{1,2},{2,3},{3,4},{4,5},{5,6},{6,7},{7,8},{8,9},{9,10},{10,1... | collective-permute-start | bytes 393224 | tf_op jit(solution)/shard_map/while/body/eval_jaxpr/ppermute | solution.py:19
  145.1 8.4 %collective-permute-start.1 = (bf16[1,128,512]{2,1,0:T(8,128)(2,1)}, bf16[1,128,512]{2,1,0:T(8,128)(2,1)}, u32[]{:S(2)}, u32[]{:S(2)}) collective-permute-start(bf16[1,128,512]{2,1,0:T(8,128)(2,1)} %copy.147), channel_id=1, source_target_pairs={{0,1},{1,2},{2,3},{3,4},{4,5},{5,6},{6,7},{7,8},{8,9},{9,10},{10,1... | collective-permute-start | bytes 393224 | tf_op jit(solution)/shard_map/while/body/eval_jaxpr/ppermute | solution.py:19
  151.1 9.8 %collective-permute-start.2 = (f32[1,128,512]{1,2,0:T(8,128)}, f32[1,128,512]{1,2,0:T(8,128)}, u32[]{:S(2)}, u32[]{:S(2)}) collective-permute-start(f32[1,128,512]{1,2,0:T(8,128)} %add.356), channel_id=1, source_target_pairs={{0,1},{1,2},{2,3},{3,4},{4,5},{5,6},{6,7},{7,8},{8,9},{9,10},{10,1... | collective-permute-start | bytes 786440 | tf_op jit(solution)/shard_map/while/body/eval_jaxpr/ppermute | solution.py:19
  153.1 10.6 %collective-permute-start.3 = (f32[1,128,512]{1,2,0:T(8,128)}, f32[1,128,512]{1,2,0:T(8,128)}, u32[]{:S(2)}, u32[]{:S(2)}) collective-permute-start(f32[1,128,512]{1,2,0:T(8,128)} %add.357), channel_id=1, source_target_pairs={{0,1},{1,2},{2,3},{3,4},{4,5},{5,6},{6,7},{7,8},{8,9},{9,10},{10,1... | collective-permute-start | bytes 786440 | tf_op jit(solution)/shard_map/while/body/eval_jaxpr/ppermute | solution.py:19
  164.5 10.0 %collective-permute-start = (bf16[1,128,512]{2,1,0:T(8,128)(2,1)S(1)}, bf16[1,128,512]{2,1,0:T(8,128)(2,1)}, u32[]{:S(2)}, u32[]{:S(2)}) collective-permute-start(bf16[1,128,512]{2,1,0:T(8,128)(2,1)S(1)} %copy.146), channel_id=1, source_target_pairs={{0,1},{1,2},{2,3},{3,4},{4,5},{5,6},{6,7},{7,8},{8,9},{9,10},{10,1... | collective-permute-start | bytes 393224 | tf_op jit(solution)/shard_map/while/body/eval_jaxpr/ppermute | solution.py:19
  166.1 8.4 %collective-permute-start.1 = (bf16[1,128,512]{2,1,0:T(8,128)(2,1)}, bf16[1,128,512]{2,1,0:T(8,128)(2,1)}, u32[]{:S(2)}, u32[]{:S(2)}) collective-permute-start(bf16[1,128,512]{2,1,0:T(8,128)(2,1)} %copy.147), channel_id=1, source_target_pairs={{0,1},{1,2},{2,3},{3,4},{4,5},{5,6},{6,7},{7,8},{8,9},{9,10},{10,1... | collective-permute-start | bytes 393224 | tf_op jit(solution)/shard_map/while/body/eval_jaxpr/ppermute | solution.py:19
  172.0 9.8 %collective-permute-start.2 = (f32[1,128,512]{1,2,0:T(8,128)}, f32[1,128,512]{1,2,0:T(8,128)}, u32[]{:S(2)}, u32[]{:S(2)}) collective-permute-start(f32[1,128,512]{1,2,0:T(8,128)} %add.356), channel_id=1, source_target_pairs={{0,1},{1,2},{2,3},{3,4},{4,5},{5,6},{6,7},{7,8},{8,9},{9,10},{10,1... | collective-permute-start | bytes 786440 | tf_op jit(solution)/shard_map/while/body/eval_jaxpr/ppermute | solution.py:19
  174.0 10.6 %collective-permute-start.3 = (f32[1,128,512]{1,2,0:T(8,128)}, f32[1,128,512]{1,2,0:T(8,128)}, u32[]{:S(2)}, u32[]{:S(2)}) collective-permute-start(f32[1,128,512]{1,2,0:T(8,128)} %add.357), channel_id=1, source_target_pairs={{0,1},{1,2},{2,3},{3,4},{4,5},{5,6},{6,7},{7,8},{8,9},{9,10},{10,1... | collective-permute-start | bytes 786440 | tf_op jit(solution)/shard_map/while/body/eval_jaxpr/ppermute | solution.py:19
  185.5 10.0 %collective-permute-start = (bf16[1,128,512]{2,1,0:T(8,128)(2,1)S(1)}, bf16[1,128,512]{2,1,0:T(8,128)(2,1)}, u32[]{:S(2)}, u32[]{:S(2)}) collective-permute-start(bf16[1,128,512]{2,1,0:T(8,128)(2,1)S(1)} %copy.146), channel_id=1, source_target_pairs={{0,1},{1,2},{2,3},{3,4},{4,5},{5,6},{6,7},{7,8},{8,9},{9,10},{10,1... | collective-permute-start | bytes 393224 | tf_op jit(solution)/shard_map/while/body/eval_jaxpr/ppermute | solution.py:19
  187.1 8.4 %collective-permute-start.1 = (bf16[1,128,512]{2,1,0:T(8,128)(2,1)}, bf16[1,128,512]{2,1,0:T(8,128)(2,1)}, u32[]{:S(2)}, u32[]{:S(2)}) collective-permute-start(bf16[1,128,512]{2,1,0:T(8,128)(2,1)} %copy.147), channel_id=1, source_target_pairs={{0,1},{1,2},{2,3},{3,4},{4,5},{5,6},{6,7},{7,8},{8,9},{9,10},{10,1... | collective-permute-start | bytes 393224 | tf_op jit(solution)/shard_map/while/body/eval_jaxpr/ppermute | solution.py:19
  193.0 9.8 %collective-permute-start.2 = (f32[1,128,512]{1,2,0:T(8,128)}, f32[1,128,512]{1,2,0:T(8,128)}, u32[]{:S(2)}, u32[]{:S(2)}) collective-permute-start(f32[1,128,512]{1,2,0:T(8,128)} %add.356), channel_id=1, source_target_pairs={{0,1},{1,2},{2,3},{3,4},{4,5},{5,6},{6,7},{7,8},{8,9},{9,10},{10,1... | collective-permute-start | bytes 786440 | tf_op jit(solution)/shard_map/while/body/eval_jaxpr/ppermute | solution.py:19
  195.0 10.6 %collective-permute-start.3 = (f32[1,128,512]{1,2,0:T(8,128)}, f32[1,128,512]{1,2,0:T(8,128)}, u32[]{:S(2)}, u32[]{:S(2)}) collective-permute-start(f32[1,128,512]{1,2,0:T(8,128)} %add.357), channel_id=1, source_target_pairs={{0,1},{1,2},{2,3},{3,4},{4,5},{5,6},{6,7},{7,8},{8,9},{9,10},{10,1... | collective-permute-start | bytes 786440 | tf_op jit(solution)/shard_map/while/body/eval_jaxpr/ppermute | solution.py:19
  206.5 10.0 %collective-permute-start = (bf16[1,128,512]{2,1,0:T(8,128)(2,1)S(1)}, bf16[1,128,512]{2,1,0:T(8,128)(2,1)}, u32[]{:S(2)}, u32[]{:S(2)}) collective-permute-start(bf16[1,128,512]{2,1,0:T(8,128)(2,1)S(1)} %copy.146), channel_id=1, source_target_pairs={{0,1},{1,2},{2,3},{3,4},{4,5},{5,6},{6,7},{7,8},{8,9},{9,10},{10,1... | collective-permute-start | bytes 393224 | tf_op jit(solution)/shard_map/while/body/eval_jaxpr/ppermute | solution.py:19
  208.0 8.4 %collective-permute-start.1 = (bf16[1,128,512]{2,1,0:T(8,128)(2,1)}, bf16[1,128,512]{2,1,0:T(8,128)(2,1)}, u32[]{:S(2)}, u32[]{:S(2)}) collective-permute-start(bf16[1,128,512]{2,1,0:T(8,128)(2,1)} %copy.147), channel_id=1, source_target_pairs={{0,1},{1,2},{2,3},{3,4},{4,5},{5,6},{6,7},{7,8},{8,9},{9,10},{10,1... | collective-permute-start | bytes 393224 | tf_op jit(solution)/shard_map/while/body/eval_jaxpr/ppermute | solution.py:19
  213.9 9.8 %collective-permute-start.2 = (f32[1,128,512]{1,2,0:T(8,128)}, f32[1,128,512]{1,2,0:T(8,128)}, u32[]{:S(2)}, u32[]{:S(2)}) collective-permute-start(f32[1,128,512]{1,2,0:T(8,128)} %add.356), channel_id=1, source_target_pairs={{0,1},{1,2},{2,3},{3,4},{4,5},{5,6},{6,7},{7,8},{8,9},{9,10},{10,1... | collective-permute-start | bytes 786440 | tf_op jit(solution)/shard_map/while/body/eval_jaxpr/ppermute | solution.py:19
  215.9 10.6 %collective-permute-start.3 = (f32[1,128,512]{1,2,0:T(8,128)}, f32[1,128,512]{1,2,0:T(8,128)}, u32[]{:S(2)}, u32[]{:S(2)}) collective-permute-start(f32[1,128,512]{1,2,0:T(8,128)} %add.357), channel_id=1, source_target_pairs={{0,1},{1,2},{2,3},{3,4},{4,5},{5,6},{6,7},{7,8},{8,9},{9,10},{10,1... | collective-permute-start | bytes 786440 | tf_op jit(solution)/shard_map/while/body/eval_jaxpr/ppermute | solution.py:19
  227.4 10.0 %collective-permute-start = (bf16[1,128,512]{2,1,0:T(8,128)(2,1)S(1)}, bf16[1,128,512]{2,1,0:T(8,128)(2,1)}, u32[]{:S(2)}, u32[]{:S(2)}) collective-permute-start(bf16[1,128,512]{2,1,0:T(8,128)(2,1)S(1)} %copy.146), channel_id=1, source_target_pairs={{0,1},{1,2},{2,3},{3,4},{4,5},{5,6},{6,7},{7,8},{8,9},{9,10},{10,1... | collective-permute-start | bytes 393224 | tf_op jit(solution)/shard_map/while/body/eval_jaxpr/ppermute | solution.py:19
  229.0 8.4 %collective-permute-start.1 = (bf16[1,128,512]{2,1,0:T(8,128)(2,1)}, bf16[1,128,512]{2,1,0:T(8,128)(2,1)}, u32[]{:S(2)}, u32[]{:S(2)}) collective-permute-start(bf16[1,128,512]{2,1,0:T(8,128)(2,1)} %copy.147), channel_id=1, source_target_pairs={{0,1},{1,2},{2,3},{3,4},{4,5},{5,6},{6,7},{7,8},{8,9},{9,10},{10,1... | collective-permute-start | bytes 393224 | tf_op jit(solution)/shard_map/while/body/eval_jaxpr/ppermute | solution.py:19
  234.9 9.8 %collective-permute-start.2 = (f32[1,128,512]{1,2,0:T(8,128)}, f32[1,128,512]{1,2,0:T(8,128)}, u32[]{:S(2)}, u32[]{:S(2)}) collective-permute-start(f32[1,128,512]{1,2,0:T(8,128)} %add.356), channel_id=1, source_target_pairs={{0,1},{1,2},{2,3},{3,4},{4,5},{5,6},{6,7},{7,8},{8,9},{9,10},{10,1... | collective-permute-start | bytes 786440 | tf_op jit(solution)/shard_map/while/body/eval_jaxpr/ppermute | solution.py:19
  236.9 10.6 %collective-permute-start.3 = (f32[1,128,512]{1,2,0:T(8,128)}, f32[1,128,512]{1,2,0:T(8,128)}, u32[]{:S(2)}, u32[]{:S(2)}) collective-permute-start(f32[1,128,512]{1,2,0:T(8,128)} %add.357), channel_id=1, source_target_pairs={{0,1},{1,2},{2,3},{3,4},{4,5},{5,6},{6,7},{7,8},{8,9},{9,10},{10,1... | collective-permute-start | bytes 786440 | tf_op jit(solution)/shard_map/while/body/eval_jaxpr/ppermute | solution.py:19
  248.4 10.0 %collective-permute-start = (bf16[1,128,512]{2,1,0:T(8,128)(2,1)S(1)}, bf16[1,128,512]{2,1,0:T(8,128)(2,1)}, u32[]{:S(2)}, u32[]{:S(2)}) collective-permute-start(bf16[1,128,512]{2,1,0:T(8,128)(2,1)S(1)} %copy.146), channel_id=1, source_target_pairs={{0,1},{1,2},{2,3},{3,4},{4,5},{5,6},{6,7},{7,8},{8,9},{9,10},{10,1... | collective-permute-start | bytes 393224 | tf_op jit(solution)/shard_map/while/body/eval_jaxpr/ppermute | solution.py:19
  249.9 8.4 %collective-permute-start.1 = (bf16[1,128,512]{2,1,0:T(8,128)(2,1)}, bf16[1,128,512]{2,1,0:T(8,128)(2,1)}, u32[]{:S(2)}, u32[]{:S(2)}) collective-permute-start(bf16[1,128,512]{2,1,0:T(8,128)(2,1)} %copy.147), channel_id=1, source_target_pairs={{0,1},{1,2},{2,3},{3,4},{4,5},{5,6},{6,7},{7,8},{8,9},{9,10},{10,1... | collective-permute-start | bytes 393224 | tf_op jit(solution)/shard_map/while/body/eval_jaxpr/ppermute | solution.py:19
  255.9 9.8 %collective-permute-start.2 = (f32[1,128,512]{1,2,0:T(8,128)}, f32[1,128,512]{1,2,0:T(8,128)}, u32[]{:S(2)}, u32[]{:S(2)}) collective-permute-start(f32[1,128,512]{1,2,0:T(8,128)} %add.356), channel_id=1, source_target_pairs={{0,1},{1,2},{2,3},{3,4},{4,5},{5,6},{6,7},{7,8},{8,9},{9,10},{10,1... | collective-permute-start | bytes 786440 | tf_op jit(solution)/shard_map/while/body/eval_jaxpr/ppermute | solution.py:19
  257.9 10.6 %collective-permute-start.3 = (f32[1,128,512]{1,2,0:T(8,128)}, f32[1,128,512]{1,2,0:T(8,128)}, u32[]{:S(2)}, u32[]{:S(2)}) collective-permute-start(f32[1,128,512]{1,2,0:T(8,128)} %add.357), channel_id=1, source_target_pairs={{0,1},{1,2},{2,3},{3,4},{4,5},{5,6},{6,7},{7,8},{8,9},{9,10},{10,1... | collective-permute-start | bytes 786440 | tf_op jit(solution)/shard_map/while/body/eval_jaxpr/ppermute | solution.py:19
  269.3 10.0 %collective-permute-start = (bf16[1,128,512]{2,1,0:T(8,128)(2,1)S(1)}, bf16[1,128,512]{2,1,0:T(8,128)(2,1)}, u32[]{:S(2)}, u32[]{:S(2)}) collective-permute-start(bf16[1,128,512]{2,1,0:T(8,128)(2,1)S(1)} %copy.146), channel_id=1, source_target_pairs={{0,1},{1,2},{2,3},{3,4},{4,5},{5,6},{6,7},{7,8},{8,9},{9,10},{10,1... | collective-permute-start | bytes 393224 | tf_op jit(solution)/shard_map/while/body/eval_jaxpr/ppermute | solution.py:19
  270.9 8.4 %collective-permute-start.1 = (bf16[1,128,512]{2,1,0:T(8,128)(2,1)}, bf16[1,128,512]{2,1,0:T(8,128)(2,1)}, u32[]{:S(2)}, u32[]{:S(2)}) collective-permute-start(bf16[1,128,512]{2,1,0:T(8,128)(2,1)} %copy.147), channel_id=1, source_target_pairs={{0,1},{1,2},{2,3},{3,4},{4,5},{5,6},{6,7},{7,8},{8,9},{9,10},{10,1... | collective-permute-start | bytes 393224 | tf_op jit(solution)/shard_map/while/body/eval_jaxpr/ppermute | solution.py:19
  276.8 9.8 %collective-permute-start.2 = (f32[1,128,512]{1,2,0:T(8,128)}, f32[1,128,512]{1,2,0:T(8,128)}, u32[]{:S(2)}, u32[]{:S(2)}) collective-permute-start(f32[1,128,512]{1,2,0:T(8,128)} %add.356), channel_id=1, source_target_pairs={{0,1},{1,2},{2,3},{3,4},{4,5},{5,6},{6,7},{7,8},{8,9},{9,10},{10,1... | collective-permute-start | bytes 786440 | tf_op jit(solution)/shard_map/while/body/eval_jaxpr/ppermute | solution.py:19
  278.8 10.6 %collective-permute-start.3 = (f32[1,128,512]{1,2,0:T(8,128)}, f32[1,128,512]{1,2,0:T(8,128)}, u32[]{:S(2)}, u32[]{:S(2)}) collective-permute-start(f32[1,128,512]{1,2,0:T(8,128)} %add.357), channel_id=1, source_target_pairs={{0,1},{1,2},{2,3},{3,4},{4,5},{5,6},{6,7},{7,8},{8,9},{9,10},{10,1... | collective-permute-start | bytes 786440 | tf_op jit(solution)/shard_map/while/body/eval_jaxpr/ppermute | solution.py:19
  290.3 10.0 %collective-permute-start = (bf16[1,128,512]{2,1,0:T(8,128)(2,1)S(1)}, bf16[1,128,512]{2,1,0:T(8,128)(2,1)}, u32[]{:S(2)}, u32[]{:S(2)}) collective-permute-start(bf16[1,128,512]{2,1,0:T(8,128)(2,1)S(1)} %copy.146), channel_id=1, source_target_pairs={{0,1},{1,2},{2,3},{3,4},{4,5},{5,6},{6,7},{7,8},{8,9},{9,10},{10,1... | collective-permute-start | bytes 393224 | tf_op jit(solution)/shard_map/while/body/eval_jaxpr/ppermute | solution.py:19
  291.9 8.4 %collective-permute-start.1 = (bf16[1,128,512]{2,1,0:T(8,128)(2,1)}, bf16[1,128,512]{2,1,0:T(8,128)(2,1)}, u32[]{:S(2)}, u32[]{:S(2)}) collective-permute-start(bf16[1,128,512]{2,1,0:T(8,128)(2,1)} %copy.147), channel_id=1, source_target_pairs={{0,1},{1,2},{2,3},{3,4},{4,5},{5,6},{6,7},{7,8},{8,9},{9,10},{10,1... | collective-permute-start | bytes 393224 | tf_op jit(solution)/shard_map/while/body/eval_jaxpr/ppermute | solution.py:19
  297.8 9.8 %collective-permute-start.2 = (f32[1,128,512]{1,2,0:T(8,128)}, f32[1,128,512]{1,2,0:T(8,128)}, u32[]{:S(2)}, u32[]{:S(2)}) collective-permute-start(f32[1,128,512]{1,2,0:T(8,128)} %add.356), channel_id=1, source_target_pairs={{0,1},{1,2},{2,3},{3,4},{4,5},{5,6},{6,7},{7,8},{8,9},{9,10},{10,1... | collective-permute-start | bytes 786440 | tf_op jit(solution)/shard_map/while/body/eval_jaxpr/ppermute | solution.py:19
  299.8 10.6 %collective-permute-start.3 = (f32[1,128,512]{1,2,0:T(8,128)}, f32[1,128,512]{1,2,0:T(8,128)}, u32[]{:S(2)}, u32[]{:S(2)}) collective-permute-start(f32[1,128,512]{1,2,0:T(8,128)} %add.357), channel_id=1, source_target_pairs={{0,1},{1,2},{2,3},{3,4},{4,5},{5,6},{6,7},{7,8},{8,9},{9,10},{10,1... | collective-permute-start | bytes 786440 | tf_op jit(solution)/shard_map/while/body/eval_jaxpr/ppermute | solution.py:19
  311.3 10.0 %collective-permute-start = (bf16[1,128,512]{2,1,0:T(8,128)(2,1)S(1)}, bf16[1,128,512]{2,1,0:T(8,128)(2,1)}, u32[]{:S(2)}, u32[]{:S(2)}) collective-permute-start(bf16[1,128,512]{2,1,0:T(8,128)(2,1)S(1)} %copy.146), channel_id=1, source_target_pairs={{0,1},{1,2},{2,3},{3,4},{4,5},{5,6},{6,7},{7,8},{8,9},{9,10},{10,1... | collective-permute-start | bytes 393224 | tf_op jit(solution)/shard_map/while/body/eval_jaxpr/ppermute | solution.py:19
  312.8 8.4 %collective-permute-start.1 = (bf16[1,128,512]{2,1,0:T(8,128)(2,1)}, bf16[1,128,512]{2,1,0:T(8,128)(2,1)}, u32[]{:S(2)}, u32[]{:S(2)}) collective-permute-start(bf16[1,128,512]{2,1,0:T(8,128)(2,1)} %copy.147), channel_id=1, source_target_pairs={{0,1},{1,2},{2,3},{3,4},{4,5},{5,6},{6,7},{7,8},{8,9},{9,10},{10,1... | collective-permute-start | bytes 393224 | tf_op jit(solution)/shard_map/while/body/eval_jaxpr/ppermute | solution.py:19
  318.7 9.8 %collective-permute-start.2 = (f32[1,128,512]{1,2,0:T(8,128)}, f32[1,128,512]{1,2,0:T(8,128)}, u32[]{:S(2)}, u32[]{:S(2)}) collective-permute-start(f32[1,128,512]{1,2,0:T(8,128)} %add.356), channel_id=1, source_target_pairs={{0,1},{1,2},{2,3},{3,4},{4,5},{5,6},{6,7},{7,8},{8,9},{9,10},{10,1... | collective-permute-start | bytes 786440 | tf_op jit(solution)/shard_map/while/body/eval_jaxpr/ppermute | solution.py:19
  320.7 10.6 %collective-permute-start.3 = (f32[1,128,512]{1,2,0:T(8,128)}, f32[1,128,512]{1,2,0:T(8,128)}, u32[]{:S(2)}, u32[]{:S(2)}) collective-permute-start(f32[1,128,512]{1,2,0:T(8,128)} %add.357), channel_id=1, source_target_pairs={{0,1},{1,2},{2,3},{3,4},{4,5},{5,6},{6,7},{7,8},{8,9},{9,10},{10,1... | collective-permute-start | bytes 786440 | tf_op jit(solution)/shard_map/while/body/eval_jaxpr/ppermute | solution.py:19
  339.5 8.2 %collective-permute-start.4 = (bf16[1,128,512]{2,1,0:T(8,128)(2,1)}, bf16[1,128,512]{2,1,0:T(8,128)(2,1)S(1)}, u32[]{:S(2)}, u32[]{:S(2)}) collective-permute-start(bf16[1,128,512]{2,1,0:T(8,128)(2,1)} %add.231), channel_id=1, source_target_pairs={{0,1},{1,2},{2,3},{3,4},{4,5},{5,6},{6,7},{7,8},{8,9},{9,10},{10,1... | collective-permute-start | bytes 393224 | tf_op jit(solution)/shard_map/ppermute | solution.py:19
  342.3 8.1 %collective-permute-start.5 = (bf16[1,128,512]{2,1,0:T(8,128)(2,1)S(1)}, bf16[1,128,512]{2,1,0:T(8,128)(2,1)S(1)}, u32[]{:S(2)}, u32[]{:S(2)}) collective-permute-start(bf16[1,128,512]{2,1,0:T(8,128)(2,1)S(1)} %add.232), channel_id=1, source_target_pairs={{0,1},{1,2},{2,3},{3,4},{4,5},{5,6},{6,7},{7,8},{8,9},{9,10},{10,1... | collective-permute-start | bytes 393224 | tf_op jit(solution)/shard_map/ppermute | solution.py:19
  457.6 18.6 %all-to-all-start = ((f32[16,8,1024]{2,1,0:T(8,128)}), f32[16,8,1024]{2,1,0:T(8,128)}, u32[]{:S(2)}, u32[]{:S(2)}) async-start(f32[16,8,1024]{2,1,0:T(8,128)} %bitcast.31), calls=%async_computation.1 | async-start | bytes 1048576 | tf_op jit(solution)/shard_map/all_to_all | solution.py:30
  (2 other events, 344.5 us)
Sparse Core Ops, SparseCore 0:
  355.0 100.5 reduce-scatter.1
where the time goes:
time: 491 us; the launch traced here: 486 us
  waiting for transfers between devices  269 us (55%)
  local copies, waits for them, and re-layouts  69.4 us (14%)
  other arithmetic  67.2 us (14%)
  matrix products  55.4 us (11%)
  between operations  14.2 us (3%)
  starting transfers between devices  9.9 us (2%)
    ppermute x62, waiting for transfers between devices, passed_along(): return lax.ppermute(value, axis, pairs)  157 us
    reduce_scatter x1, waiting for transfers between devices, shards(): lax.psum_scatter(jnp.einsum('td,te->de', flat_hidden, token_grads, prefer...  101 us
    add x32, other arithmetic, block_grads(): return (key_acc + key_part, value_acc + value_part, query_acc + query_part)  52.4 us
    while x30, local copies, waits for them, and re-layouts  37.1 us
    dot_general x32, matrix products, head_scores(): jnp.einsum('bqhgd,bkhd->bhgqk', left_heads, right_heads, preferred_elemen...  32.8 us
    another operation x33, local copies, waits for them, and re-layouts  16.7 us
    reduce_sum x16, other arithmetic, stored_positions(): block_ids = jnp.sum(jnp.where(matches, block_order[None, :], 0), axis=1)  11.9 us
    all_to_all x1, waiting for transfers between devices, summed_on_arrival(): lax.all_to_all(parts, axis, split_axis=0, concat_axis=0, tiled=True)  10.7 us
  transfers between devices with their start and end apart: 64, of which 34 were waited for; matrix products, arithmetic and copies ran while one was open for 31% of the time, Pallas kernels for 0%

commit v1 on v0

v1 whole, which is shorter than its diff:
```python
import functools
import math

import jax
import jax.numpy as jnp
from jax import lax
from jax.experimental import pallas as pl
from jax.experimental.pallas import tpu as pltpu
from jax.sharding import PartitionSpec as P

MESH = pl.DeviceIdType.MESH
HQ = 16
HK = 4
DH = 128
SCALE = 1.0 / math.sqrt(DH)
LOG2E = math.log2(math.e)
BF = jnp.bfloat16
F32 = jnp.float32


def place():
    b, s = lax.axis_index("batch"), lax.axis_index("seq")
    return b, s, s // 8, (s // 2) % 4, s % 2


def seq_of(xh, y, c):
    return xh * 8 + y * 2 + c


def near(b, xh, y, c):
    along = [(b, seq_of(xh, (y + d) % 4, c)) for d in (1, 2, 3)]
    return along, (b, seq_of(xh, y, 1 - c)), (b, seq_of(1 - xh, y, c))


def remote(src, dst, send, recv, dev):
    copy = pltpu.make_async_remote_copy(
        src_ref=src,
        dst_ref=dst,
        send_sem=send,
        recv_sem=recv,
        device_id=dev,
        device_id_type=MESH,
    )
    copy.start()
    return copy


def signal(sem, dev):
    pl.semaphore_signal(sem, inc=1, device_id=dev, device_id_type=MESH)


def lanes(index, width):
    return pl.ds(pl.multiple_of(index * width, width), width)


def gather_kernel(q, do, k, v, ld, qx, dox, kvx, ldx, ssem, rsem, lsem):
    b, s, xh, y, c = place()
    along, partner, across = near(b, xh, y, c)
    barrier = pltpu.get_barrier_semaphore()
    for dev in (*along, partner, across):
        signal(barrier, dev)
    pl.semaphore_wait(barrier, 5)

    own_k = pltpu.make_async_copy(k.at[:, lanes(y, 128)], kvx.at[0, 0, :, pl.ds(0, 128)], lsem.at[0])
    own_v = pltpu.make_async_copy(v.at[:, lanes(y, 128)], kvx.at[0, 0, :, pl.ds(128, 128)], lsem.at[1])
    own_k.start()
    own_v.start()
    kv, rest = [], []
    for d in (2, 1, 3):
        t, dev = (y + d) % 4, along[d - 1]
        kv.append(remote(k.at[:, lanes(t, 128)], kvx.at[0, d, :, pl.ds(0, 128)], ssem.at[0, d], rsem.at[0, d], dev))
        kv.append(remote(v.at[:, lanes(t, 128)], kvx.at[0, d, :, pl.ds(128, 128)], ssem.at[1, d], rsem.at[1, d], dev))
    for d in (2, 1, 3):
        t, dev = (y + d) % 4, along[d - 1]
        rest.append(remote(ld.at[t], ldx.at[d - 1], ssem.at[2, d], rsem.at[2, d], dev))
        rest.append(remote(q.at[:, lanes(t, 512)], qx.at[d - 1], ssem.at[3, d], rsem.at[3, d], dev))
        rest.append(remote(do.at[:, lanes(t, 512)], dox.at[d - 1], ssem.at[4, d], rsem.at[4, d], dev))
    own_k.wait()
    own_v.wait()
    for copy in kv:
        copy.wait_recv()
    far = remote(kvx.at[0], kvx.at[2], ssem.at[0, 0], rsem.at[0, 0], across)
    side = remote(kvx.at[0], kvx.at[1], ssem.at[1, 0], rsem.at[1, 0], partner)
    far.wait_recv()
    last = remote(kvx.at[2], kvx.at[3], ssem.at[2, 0], rsem.at[2, 0], partner)
    for copy in kv:
        copy.wait_send()
    for copy in rest:
        copy.wait()
    far.wait_send()
    side.wait()
    last.wait()


def attention_kernel(order, q, do, ld, qx, dox, ldx, kvx, dqx, dkv, ks, vs, kt, qs, dos, lds, dka, dva, dqt):
    b, s, xh, y, c = place()

    def stored(m, d):
        return seq_of(xh ^ (m >> 1), (y + 4 - d) % 4, c ^ (m & 1))

    def rows(block):
        return pl.ds(pl.multiple_of(block * 64, 64), 64)

    for m in range(4):
        for d in range(4):
            for half in range(2):
                to = rows(order[stored(m, d) * 2 + half])
                ks[to, :] = kvx[m, d, half * 64 : half * 64 + 64, 0:128]
                vs[to, :] = kvx[m, d, half * 64 : half * 64 + 64, 128:256]
    for n in range(8):
        kt[n] = ks[n * 256 : n * 256 + 256, :].T
    for d in range(4):
        for half in range(2):
            for h in range(4):
                at = (slice(half * 64, half * 64 + 64), slice(h * 128, h * 128 + 128))
                if d:
                    qs[d * 2 + half, h * 64 : h * 64 + 64, :] = qx[(d - 1, *at)]
                    dos[d * 2 + half, h * 64 : h * 64 + 64, :] = dox[(d - 1, *at)]
                else:
                    own = lanes(y * 4 + h, 128)
                    qs[half, h * 64 : h * 64 + 64, :] = q[half * 64 : half * 64 + 64, own]
                    dos[half, h * 64 : h * 64 + 64, :] = do[half * 64 : half * 64 + 64, own]
        lds[d] = ldx[d - 1] if d else ld[y]
    dka[...] = jnp.zeros_like(dka)
    dva[...] = jnp.zeros_like(dva)
    gap = (
        lax.broadcasted_iota(jnp.int32, (256, 256), 0)
        - lax.broadcasted_iota(jnp.int32, (256, 256), 1) % 64
    )

    def piece(d, i):
        first = order[stored(0, d) * 2]
        turn = first // 4 + 1
        half = jnp.where(i < turn, 0, 1)
        n = jnp.where(i < turn, i, i - turn)
        block = jnp.where(i < turn, first, 31 - first)
        keys = pl.ds(pl.multiple_of(n * 256, 256), 256)
        qb, dob = qs[d * 2 + half], dos[d * 2 + half]
        base = half * 4
        lse = jnp.concatenate([lds[d, pl.ds(base, 1), :], lds[d, pl.ds(base + 1, 1), :]], axis=1)
        delta = jnp.concatenate([lds[d, pl.ds(base + 2, 1), :], lds[d, pl.ds(base + 3, 1), :]], axis=1)
        nt = (((1,), (1,)), ((), ()))
        scores = lax.dot_general(ks[keys, :], qb, nt, preferred_element_type=F32)
        probs = jnp.exp2(scores * (SCALE * LOG2E) - lse)
        probs = jnp.where(gap <= block * 64 - n * 256, probs, 0.0)
        dprobs = lax.dot_general(vs[keys, :], dob, nt, preferred_element_type=F32)
        dscores = (probs * (dprobs - delta) * SCALE).astype(BF)
        low = probs.astype(BF)
        dva[keys, :] += jnp.dot(low, dob, preferred_element_type=F32)
        dka[keys, :] += jnp.dot(dscores, qb, preferred_element_type=F32)
        dqt[half] += jnp.dot(kt[n], dscores, preferred_element_type=F32)

    @pl.loop(0, 4)
    def _(d):
        dqt[...] = jnp.zeros_like(dqt)

        @pl.loop(0, 3)
        def _(t):
            for u in range(3):
                piece(d, t * 3 + u)

        for half in range(2):
            dq = dqt[half].T
            for h in range(4):
                dqx[d, half * 64 : half * 64 + 64, h * 128 : h * 128 + 128] = dq[h * 64 : h * 64 + 64, :].astype(BF)

    for m in range(4):
        for d in range(4):
            for half in range(2):
                at = rows(order[stored(m, d) * 2 + half])
                dkv[m, d, half * 64 : half * 64 + 64, 0:128] = dka[at, :]
                dkv[m, d, half * 64 : half * 64 + 64, 128:256] = dva[at, :]


def reduce_kernel(
    dkv, dqx, hid, dq, dk, dv, kw, vw,
    hx, ht, sa, ra, sx, rx, g, acc, sb, rb, sy, ry, sf, rf,
    ssem, rsem, xsem, ysem, fsend, frecv, lsem,
):
    b, s, xh, y, c = place()
    along, partner, across = near(b, xh, y, c)
    quarter = xh * 2 + c
    to_b = y * 4 + quarter
    from_s = seq_of((b % 4) // 2, b // 4, b % 2)
    mine = to_b == b

    barrier = pltpu.get_barrier_semaphore()
    for dev in (*along, partner, across):
        signal(barrier, dev)

    @pl.loop(0, 16)
    def _(i):
        @pl.when(jnp.logical_not(mine & (i == s)))
        def _():
            signal(barrier, (to_b, i))

        @pl.when(jnp.logical_not(mine & (i == b)))
        def _():
            signal(barrier, (i, from_s))

    pl.semaphore_wait(barrier, jnp.where(mine, 35, 37))

    own_h = pltpu.make_async_copy(hid.at[:, lanes(y, 512)], hx.at[0], lsem.at[0])
    own_q = pltpu.make_async_copy(dqx.at[0], dq.at[:, lanes(y, 512)], lsem.at[1])
    own_h.start()
    own_q.start()
    home, feats = [], []
    for d in (2, 1, 3):
        dev = along[d - 1]
        feats.append(remote(hid.at[:, lanes((y + d) % 4, 512)], hx.at[d], ssem.at[0, d], rsem.at[0, d], dev))
    for d in (2, 1, 3):
        dev = along[(4 - d) - 1]
        home.append(remote(dqx.at[d], dq.at[:, lanes(y, 512)], ssem.at[1, d], rsem.at[1, d], dev))

    def summed(part, send, recv, send_far, recv_far, sems):
        send[1] = part(3).astype(BF)
        one = remote(send.at[1], recv.at[1], sems.at[0, 0], sems.at[0, 1], partner)
        send[0] = part(1).astype(BF)
        two = remote(send.at[0], recv.at[0], sems.at[1, 0], sems.at[1, 1], partner)
        one.wait_recv()
        send_far[...] = (part(2) + recv[1].astype(F32)).astype(BF)
        far = remote(send_far, recv_far, sems.at[2, 0], sems.at[2, 1], across)
        two.wait_recv()
        far.wait_recv()
        total = part(0) + recv[0].astype(F32) + recv_far[...].astype(F32)
        one.wait_send()
        two.wait_send()
        far.wait_send()
        return total

    g[0] = summed(lambda m: dkv[m], sa, ra, sx, rx, xsem).astype(BF)
    grads = {}
    for e in (2, 1, 3):
        grads[e] = remote(g.at[0], g.at[e], ssem.at[2, e], rsem.at[2, e], along[e - 1])
    own_h.wait()
    for copy in feats:
        copy.wait()
    for d in range(4):
        ht[:, d * 128 : d * 128 + 128] = hx[d].T
    for e in (0, 1, 3, 2):
        if e:
            grads[e].wait_recv()
        head = (y + 4 - e) % 4
        own = (4 - e) % 4
        dk[:, lanes(head, 128)] = g[e, own, :, 0:128]
        dv[:, lanes(head, 128)] = g[e, own, :, 128:256]
        tokens = jnp.concatenate([g[e, (d + 4 - e) % 4] for d in range(4)], axis=0)
        acc[:, lanes(head, 256)] = jnp.dot(ht[...], tokens, preferred_element_type=F32)

    def quarter_rows(m):
        at = (xh ^ (m >> 1)) * 2 + (c ^ (m & 1))
        return acc[pl.ds(pl.multiple_of(at * 128, 128), 128), :]

    total = summed(quarter_rows, sb, rb, sy, ry, ysem)
    sf[...] = total.reshape(16, 8, 1024).astype(BF)

    @pl.loop(0, 16)
    def _(i):
        is_me = mine & (i == s)

        @pl.when(is_me)
        def _():
            pltpu.make_async_copy(sf.at[i], rf.at[b], lsem.at[2]).start()

        @pl.when(jnp.logical_not(is_me))
        def _():
            remote(sf.at[i], rf.at[b], fsend.at[i], frecv.at[b], (to_b, i))

    @pl.loop(0, 16)
    def _(i):
        is_me = mine & (i == b)

        @pl.when(is_me)
        def _():
            pltpu.make_async_copy(sf.at[s], rf.at[i], lsem.at[2]).wait()

        @pl.when(jnp.logical_not(is_me))
        def _():
            pltpu.make_async_remote_copy(
                src_ref=sf.at[0], dst_ref=rf.at[i], send_sem=fsend.at[0], recv_sem=frecv.at[i],
                device_id=(i, from_s), device_id_type=MESH,
            ).wait_recv()

    rows = jnp.sum(rf[...].astype(F32), axis=0)
    for h in range(4):
        kw[:, h * 128 : h * 128 + 128] = rows[:, h * 256 : h * 256 + 128]
        vw[:, h * 128 : h * 128 + 128] = rows[:, h * 256 + 128 : h * 256 + 256]

    @pl.loop(0, 16)
    def _(i):
        @pl.when(jnp.logical_not(mine & (i == s)))
        def _():
            pltpu.make_async_remote_copy(
                src_ref=sf.at[i], dst_ref=rf.at[b], send_sem=fsend.at[i], recv_sem=frecv.at[b],
                device_id=(to_b, i), device_id_type=MESH,
            ).wait_send()

    own_q.wait()
    for copy in home:
        copy.wait()
    for e in (1, 2, 3):
        grads[e].wait_send()


VMEM = pl.BlockSpec(memory_space=pltpu.VMEM)
SMEM = pl.BlockSpec(memory_space=pltpu.SMEM)
ANY = pl.BlockSpec(memory_space=pl.ANY)


def struct(shape, dtype):
    return jax.ShapeDtypeStruct(shape, dtype)


def shards(hidden_in, queries, key_states, value_states, grad_out, log_sums, deltas, block_order):
    hid, q, do = hidden_in[0], queries[0], grad_out[0]
    k, v = key_states[0], value_states[0]
    ld = jnp.stack([log_sums[0] * LOG2E, deltas[0]]).reshape(2, HK, 2, 2, 2, 64)
    ld = ld.transpose(1, 4, 0, 2, 3, 5).reshape(HK, 8, 128)
    DMA = pltpu.SemaphoreType.DMA
    qx, dox, kvx, ldx = pl.pallas_call(
        gather_kernel,
        out_shape=(
            struct((3, 128, 512), BF),
            struct((3, 128, 512), BF),
            struct((4, 4, 128, 256), BF),
            struct((3, 8, 128), F32),
        ),
        in_specs=[ANY, ANY, VMEM, VMEM, VMEM],
        out_specs=(ANY, ANY, VMEM, VMEM),
        scratch_shapes=[DMA((5, 4)), DMA((5, 4)), DMA((2,))],
        name="gather",
        compiler_params=pltpu.CompilerParams(collective_id=0, has_side_effects=True),
    )(q, do, k, v, ld)
    dqx, dkv = pl.pallas_call(
        attention_kernel,
        out_shape=(struct((4, 128, 512), BF), struct((4, 4, 128, 256), F32)),
        in_specs=[SMEM] + [VMEM] * 7,
        out_specs=(VMEM, VMEM),
        scratch_shapes=[
            pltpu.VMEM((2048, 128), BF),
            pltpu.VMEM((2048, 128), BF),
            pltpu.VMEM((8, 128, 256), BF),
            pltpu.VMEM((8, 256, 128), BF),
            pltpu.VMEM((8, 256, 128), BF),
            pltpu.VMEM((4, 8, 128), F32),
            pltpu.VMEM((2048, 128), F32),
            pltpu.VMEM((2048, 128), F32),
            pltpu.VMEM((2, 128, 256), F32),
        ],
        name="attention",
    )(block_order, q, do, ld, qx, dox, ldx, kvx)
    dq, dk, dv, kw, vw = pl.pallas_call(
        reduce_kernel,
        out_shape=(
            struct((128, 2048), BF),
            struct((128, 512), BF),
            struct((128, 512), BF),
            struct((8, 512), F32),
            struct((8, 512), F32),
        ),
        in_specs=[VMEM] * 3,
        out_specs=(VMEM,) * 5,
        scratch_shapes=[
            pltpu.VMEM((4, 128, 512), BF),
            pltpu.VMEM((512, 512), BF),
            pltpu.VMEM((2, 4, 128, 256), BF),
            pltpu.VMEM((2, 4, 128, 256), BF),
            pltpu.VMEM((4, 128, 256), BF),
            pltpu.VMEM((4, 128, 256), BF),
            pltpu.VMEM((4, 4, 128, 256), BF),
            pltpu.VMEM((512, 1024), F32),
            pltpu.VMEM((2, 128, 1024), BF),
            pltpu.VMEM((2, 128, 1024), BF),
            pltpu.VMEM((128, 1024), BF),
            pltpu.VMEM((128, 1024), BF),
            pltpu.VMEM((16, 8, 1024), BF),
            pltpu.VMEM((16, 8, 1024), BF),
            DMA((3, 4)),
            DMA((3, 4)),
            DMA((3, 2)),
            DMA((3, 2)),
            DMA((16,)),
            DMA((16,)),
            DMA((3,)),
        ],
        name="reduce",
        compiler_params=pltpu.CompilerParams(collective_id=1, has_side_effects=True),
    )(dkv, dqx, hid)
    return (dq[None], dk[None], dv[None], kw, vw)


def solution(mesh):
    tokens, rows = P("batch", "seq", None), P("batch", None, "seq")
    return jax.shard_map(
        shards,
        mesh=mesh,
        in_specs=(tokens, tokens, tokens, tokens, tokens, rows, rows, P()),
        out_specs=(tokens, tokens, tokens, P(("batch", "seq"), None), P(("batch", "seq"), None)),
        check_vma=False,
    )
```

time: 491 us -> 123 us (0.25)
  the two profiles are of different devices: /device:TPU:2 before, /device:TPU:7 now
where the time goes in v1:
time: 123 us
  Pallas kernels  112 us (91%)
  local copies, waits for them, and re-layouts  9.23 us (8%)
    pallas_call x1, Pallas kernels, shards(): pl.pallas_call(reduce_kernel, out_shape=(struct((128, 2048), BF), struct(...  73.1 us
    pallas_call x1, Pallas kernels, shards(): pl.pallas_call(gather_kernel, out_shape=(struct((3, 128, 512), BF), struc...  23.4 us
    pallas_call x1, Pallas kernels, shards(): pl.pallas_call(attention_kernel, out_shape=(struct((4, 128, 512), BF), st...  15.8 us
    unnamed x5, local copies, waits for them, and re-layouts  7.66 us

profile of v1, /device:TPU:7, one launch (start us, length us, event | category | flops | bytes accessed | tf_op | source)
XLA Modules:
  0.0 122.9 jit_solution(10901894029418969281)
XLA Ops:
  0.6 0.7 broadcast_multiply_fusion
  1.3 0.1 stack.8
  1.4 0.8 stack.9
  2.2 0.7 reshape.16.ld
  2.9 23.4 %gather.1 = (bf16[3,128,512]{2,1,0:T(8,128)(2,1)}, bf16[3,128,512]{2,1,0:T(8,128)(2,1)}, bf16[4,4,128,256]{3,2,1,0:T(8,128)(2,1)}, f32[3,8,128]{2,1,0:T(8,128)}) custom-call(bf16[128,2048]{1,0:T(8,128)(2,1)} %bitcast.10, bf16[128,2048]{1,0:T(8,128)(2,1)} %bitcast.12, bf16[128,512]{1,0:T(8,128)(2,1)} %bitcast.18, bf16[128,512]{1,0:T(8,128)(2,1)} %bitcast.19, ...), custom_call_target="tpu_custom_call" | custom-call | tf_op jit(solution)/shard_map/gather/pallas_call | solution.py:320
  26.4 15.8 %attention.1 = (bf16[4,128,512]{2,1,0:T(8,128)(2,1)}, f32[4,4,128,256]{3,2,1,0:T(8,128)}) custom-call(s32[32]{0:T(128)} %order.1, bf16[128,2048]{1,0:T(8,128)(2,1)} %bitcast.11, bf16[128,2048]{1,0:T(8,128)(2,1)} %bitcast.13, f32[4,8,128]{2,1,0:T(8,128)} %reshape.16.ld, bf16[3,128,512]{2,1,0:T(8,128)(2,1)} %get-tuple-element.16.qx, ...), custom_call_target="tpu_custom_call" | custom-call | tf_op jit(solution)/shard_map/attention/pallas_call | solution.py:334
  42.2 73.1 %reduce.1 = (bf16[128,2048]{1,0:T(8,128)(2,1)}, bf16[128,512]{1,0:T(8,128)(2,1)}, bf16[128,512]{1,0:T(8,128)(2,1)}, f32[8,512]{1,0:T(8,128)}, f32[8,512]{1,0:T(8,128)}) custom-call(f32[4,4,128,256]{3,2,1,0:T(8,128)} %get-tuple-element.20.dkv, bf16[4,128,512]{2,1,0:T(8,128)(2,1)} %get-tuple-element.21.dqx, bf16[128,2048]{1,0:T(8,128)(2,1)} %bitcast.15), custom_call_target="tpu_custom_call" | custom-call | tf_op jit(solution)/shard_map/reduce/pallas_call | solution.py:352
  115.3 1.9 %copy.20 = bf16[1,128,2048]{2,1,0:T(8,128)(2,1)} copy(bf16[1,128,2048]{2,1,0:T(8,128)(2,1)} %bitcast.14) | data formatting | bytes 1048576
  117.2 1.6 %copy.21 = bf16[1,128,512]{2,1,0:T(8,128)(2,1)} copy(bf16[1,128,512]{2,1,0:T(8,128)(2,1)} %bitcast.17) | data formatting | bytes 262144
  118.7 1.6 %copy.22 = bf16[1,128,512]{2,1,0:T(8,128)(2,1)} copy(bf16[1,128,512]{2,1,0:T(8,128)(2,1)} %bitcast.16) | data formatting | bytes 262144
  120.3 1.3 %copy.23 = f32[8,512]{1,0:T(8,128)} copy(f32[8,512]{1,0:T(8,128)} %get-tuple-element.35) | data formatting | bytes 32768
  121.6 1.3 %copy.24 = f32[8,512]{1,0:T(8,128)} copy(f32[8,512]{1,0:T(8,128)} %get-tuple-element.36) | data formatting | bytes 32768
  (3 shorter events, 0.0 us)

commit v2 on v0

v2 whole, which is shorter than its diff:
```python
import math

import jax
import jax.numpy as jnp
from jax import lax
from jax.experimental import pallas as pl
from jax.experimental.pallas import tpu as pltpu
from jax.sharding import PartitionSpec as P

MESH = pl.DeviceIdType.MESH
DH = 128
SCALE = 1.0 / math.sqrt(DH)
LOG2E = math.log2(math.e)
BF = jnp.bfloat16
F32 = jnp.float32
NT = (((1,), (1,)), ((), ()))


def place():
    b, s = lax.axis_index("batch"), lax.axis_index("seq")
    return b, s, s // 8, (s // 2) % 4, s % 2


def seq_of(xh, y, c):
    return xh * 8 + y * 2 + c


def remote_copy(src, dst, send, recv, dev):
    return pltpu.make_async_remote_copy(
        src_ref=src, dst_ref=dst, send_sem=send, recv_sem=recv, device_id=dev, device_id_type=MESH
    )


def remote(*args):
    copy = remote_copy(*args)
    copy.start()
    return copy


def lanes(index, width):
    return pl.ds(pl.multiple_of(index * width, width), width)


def fused_kernel(
    order, q, do, k, v, lse, dl, hid_in, dqh, kvg, wout,
    hid, qx, dox, kvx, lx, dx, hts, ht, ks, vs, kt, qs, dos, lsv, dlv, dka, dva, dkw, dvw, ek, ev, dqt, dqx,
    sa, ra, sx, rx, gg, acc, sb, rb, sy, ry, sf, rf, wsum,
    ssem, rsem, xsem, ysem, fsend, frecv, lsem,
):
    b, s, xh, y, c = place()
    along = [None] + [(b, seq_of(xh, (y + d) % 4, c)) for d in (1, 2, 3)]
    partner, across = (b, seq_of(xh, y, 1 - c)), (b, seq_of(1 - xh, y, c))

    own = [
        pltpu.make_async_copy(k.at[:, :, lanes(y, 128)], kvx.at[pl.ds(0, 2), :, pl.ds(0, 128)], lsem.at[0]),
        pltpu.make_async_copy(v.at[:, :, lanes(y, 128)], kvx.at[pl.ds(0, 2), :, pl.ds(128, 128)], lsem.at[1]),
        pltpu.make_async_copy(q.at[:, lanes(y, 512)], qx.at[0], lsem.at[2]),
        pltpu.make_async_copy(do.at[:, lanes(y, 512)], dox.at[0], lsem.at[3]),
        pltpu.make_async_copy(lse.at[y], lx.at[0], lsem.at[4]),
        pltpu.make_async_copy(dl.at[y], dx.at[0], lsem.at[5]),
    ]
    load = pltpu.make_async_copy(hid_in, hid, lsem.at[6])
    for copy in own:
        copy.start()
    load.start()

    barrier = pltpu.get_barrier_semaphore()
    for dev in (*along[1:], partner, across):
        pl.semaphore_signal(barrier, inc=1, device_id=dev, device_id_type=MESH)

    @pl.loop(1, 16)
    def _(t):
        pl.semaphore_signal(barrier, inc=1, device_id=((b + t) % 16, s), device_id_type=MESH)

    pl.semaphore_wait(barrier, 20)

    kv = []
    for d in (2, 1, 3):
        t, to = (y + d) % 4, pl.ds(2 * d, 2)
        kv.append(remote(k.at[:, :, lanes(t, 128)], kvx.at[to, :, pl.ds(0, 128)], ssem.at[0, d], rsem.at[0, d], along[d]))
        kv.append(remote(v.at[:, :, lanes(t, 128)], kvx.at[to, :, pl.ds(128, 128)], ssem.at[1, d], rsem.at[1, d], along[d]))
    rows_in = {}
    for d in (1, 3, 2):
        t = (y + d) % 4
        rows_in[d] = [
            remote(lse.at[t], lx.at[d], ssem.at[2, d], rsem.at[2, d], along[d]),
            remote(dl.at[t], dx.at[d], ssem.at[3, d], rsem.at[3, d], along[d]),
            remote(q.at[:, lanes(t, 512)], qx.at[d], ssem.at[4, d], rsem.at[4, d], along[d]),
            remote(do.at[:, lanes(t, 512)], dox.at[d], ssem.at[5, d], rsem.at[5, d], along[d]),
        ]

    load.wait()
    row = lax.broadcasted_iota(jnp.int32, (128, 128), 0)
    col = lax.broadcasted_iota(jnp.int32, (128, 128), 1)
    wanted = (row // 64) * 64 + ((row // 8) % 4) * 16 + ((row // 32) % 2) * 8 + row % 8
    pick = jnp.where(col == wanted, 1.0, 0.0).astype(BF)
    for i in range(16):
        turned = lax.dot_general(pick, hid[:, i * 128 : i * 128 + 128], NT, preferred_element_type=F32).astype(BF)
        for p in range(4):
            hts[p * 512 + i * 32 : p * 512 + i * 32 + 32, :] = turned[p * 32 : p * 32 + 32, :]
    feats = {}
    for d in (1, 3, 2):
        feats[d] = remote(hts, ht.at[:, pl.ds(d * 128, 128)], ssem.at[6, d], rsem.at[6, d], along[d])
    ht[:, 0:128] = hts[...]

    for copy in own:
        copy.wait()
    for copy in kv:
        copy.wait_recv()
    far = remote(kvx.at[pl.ds(0, 8)], kvx.at[pl.ds(16, 8)], ssem.at[0, 0], rsem.at[0, 0], across)
    side = remote(kvx.at[pl.ds(0, 8)], kvx.at[pl.ds(8, 8)], ssem.at[1, 0], rsem.at[1, 0], partner)
    slot_of = [None] * 32
    firsts = [order[2 * i] for i in range(16)]
    for n in range(16):
        code = jnp.int32(0)
        for i in range(16):
            code = jnp.where(firsts[i] == n, 2 * i, jnp.where(firsts[i] == 31 - n, 2 * i + 1, code))
        pair, flip = code // 2, code % 2
        index = (((pair // 8) ^ xh) * 2 + ((pair % 2) ^ c)) * 8 + ((y + 4 - (pair // 2) % 4) % 4) * 2
        slot_of[n], slot_of[31 - n] = index + flip, index + 1 - flip
    far.wait_recv()
    last = remote(kvx.at[pl.ds(16, 8)], kvx.at[pl.ds(24, 8)], ssem.at[2, 0], rsem.at[2, 0], partner)
    gap = (
        lax.broadcasted_iota(jnp.int32, (256, 256), 0)
        - lax.broadcasted_iota(jnp.int32, (256, 256), 1) % 64
    )
    dka[0:1024, :] = jnp.zeros((1024, 128), F32)
    dva[0:1024, :] = jnp.zeros((1024, 128), F32)
    side.wait_recv()
    last.wait_recv()
    for n in range(32):
        both = kvx[slot_of[n]]
        ks[n // 4, n % 4 * 64 : n % 4 * 64 + 64, :] = both[:, 0:128]
        vs[n // 4, n % 4 * 64 : n % 4 * 64 + 64, :] = both[:, 128:256]
    for n in range(8):
        kt[n] = ks[n].T

    def first_of(d):
        return order[seq_of(xh, (y + 4 - d) % 4, c) * 2]

    def low_of(d):
        first = first_of(d)
        return jnp.minimum(first, 31 - first)

    def piece(h, n, block):
        scores = lax.dot_general(ks[n], qs[h], NT, preferred_element_type=F32)
        probs = jnp.exp2(scores * (SCALE * LOG2E) - lsv[h])
        if block is not None:
            probs = jnp.where(gap <= block * 64 - n * 256, probs, 0.0)
        dprobs = lax.dot_general(vs[n], dos[h], NT, preferred_element_type=F32)
        dscores = (probs * (dprobs - dlv[h]) * SCALE).astype(BF)
        return (
            jnp.dot(dscores, qs[h], preferred_element_type=F32),
            jnp.dot(probs.astype(BF), dos[h], preferred_element_type=F32),
            jnp.dot(kt[n], dscores, preferred_element_type=F32),
        )

    def home_copy(d):
        dev = (b, seq_of(xh, (y + 4 - d) % 4, c))
        return remote_copy(dqx.at[d], dqh.at[:, lanes(y, 512)], ssem.at[7, d], rsem.at[7, d], dev)

    lane = lax.broadcasted_iota(jnp.int32, (1, 128), 1) < 64

    @pl.loop(0, 4)
    def _(turn):
        d = jnp.where(turn == 2, 3, jnp.where(turn == 3, 2, turn))

        @pl.when(turn > 0)
        def _():
            dev = (b, seq_of(xh, (y + 4 - d) % 4, c))
            remote_copy(lse.at[0], lx.at[d], ssem.at[2, d], rsem.at[2, d], dev).wait_recv()
            remote_copy(dl.at[0], dx.at[d], ssem.at[3, d], rsem.at[3, d], dev).wait_recv()
            remote_copy(q.at[:, pl.ds(0, 512)], qx.at[d], ssem.at[4, d], rsem.at[4, d], dev).wait_recv()
            remote_copy(do.at[:, pl.ds(0, 512)], dox.at[d], ssem.at[5, d], rsem.at[5, d], dev).wait_recv()

        flip = first_of(d) >= 16
        low = low_of(d)
        quad = low // 4
        for source, target in ((qx, qs), (dox, dos)):
            for h in range(4):
                zero = source[d, 0:64, h * 128 : h * 128 + 128]
                one = source[d, 64:128, h * 128 : h * 128 + 128]
                target[0, h * 64 : h * 64 + 64, :] = jnp.where(flip, one, zero)
                target[1, h * 64 : h * 64 + 64, :] = jnp.where(flip, zero, one)
        for source, target, factor in ((lx, lsv, LOG2E), (dx, dlv, None)):
            plain = source[d]
            rolled = pltpu.roll(plain, 64, axis=1)
            pairs = []
            for left, right in ((plain, rolled), (rolled, plain)):
                line = jnp.concatenate(
                    [jnp.where(lane, left[h : h + 1, :], right[h + 1 : h + 2, :]) for h in (0, 2)], axis=1
                )
                pairs.append(line if factor is None else line * factor)
            target[0] = jnp.where(flip, pairs[1], pairs[0])
            target[1] = jnp.where(flip, pairs[0], pairs[1])
        dqt[...] = jnp.zeros_like(dqt)
        for n in range(4):
            dk, dv, dq = piece(1, n, None)
            dka[n * 256 : n * 256 + 256, :] += dk
            dva[n * 256 : n * 256 + 256, :] += dv
            dqt[1] += dq
        for j in range(4):
            is_low = j <= quad
            dk, dv, dq = piece(
                jnp.where(is_low, 0, 1), jnp.where(is_low, j, 7 - j), jnp.where(is_low, low, 31 - low)
            )
            ek[d * 5 + j] = dk
            ev[d * 5 + j] = dv
            dqt[0] += jnp.where(is_low, dq, 0.0)
            dqt[1] += jnp.where(is_low, 0.0, dq)
        dk, dv, dq = piece(1, 7 - quad, 31 - low)
        ek[d * 5 + 4] = dk
        ev[d * 5 + 4] = dv
        dqt[1] += dq
        low_q, high_q = dqt[0].T, dqt[1].T
        for h in range(4):
            lo, hi = low_q[h * 64 : h * 64 + 64, :].astype(BF), high_q[h * 64 : h * 64 + 64, :].astype(BF)
            dqx[d, 0:64, h * 128 : h * 128 + 128] = jnp.where(flip, hi, lo)
            dqx[d, 64:128, h * 128 : h * 128 + 128] = jnp.where(flip, lo, hi)

        @pl.when(turn > 0)
        def _():
            home_copy(d).start()

    own_q = pltpu.make_async_copy(dqx.at[0], dqh.at[:, lanes(y, 512)], lsem.at[0])
    own_q.start()
    quads = [low_of(d) // 4 for d in range(4)]

    @pl.loop(0, 4)
    def _(part):
        for n in range(8):
            at = pl.ds(pl.multiple_of(n * 256 + part * 64, 64), 64)
            sub = pl.ds(pl.multiple_of(part * 64, 64), 64)
            for store, extra, whole in ((dka, ek, dkw), (dva, ev, dvw)):
                total = store[at, :] if n < 4 else jnp.zeros((64, 128), F32)
                for d in range(4):
                    if n < 4:
                        total += jnp.where(n <= quads[d], extra[d * 5 + n, sub, :], 0.0)
                    else:
                        total += jnp.where(7 - n > quads[d], extra[d * 5 + 7 - n, sub, :], 0.0)
                        total += jnp.where(7 - n == quads[d], extra[d * 5 + 4, sub, :], 0.0)
                whole[n * 4 + part] = total

    def summed(part, put, send, recv, send_far, recv_far, sems):
        blocks = [slice(i * 64, i * 64 + 64) for i in range(8)]
        for i in range(8):
            send[1, blocks[i], :] = part(3, i).astype(BF)
        one = remote(send.at[1], recv.at[1], sems.at[0, 0], sems.at[0, 1], partner)
        for i in range(8):
            send[0, blocks[i], :] = part(1, i).astype(BF)
        two = remote(send.at[0], recv.at[0], sems.at[1, 0], sems.at[1, 1], partner)
        one.wait_recv()
        for i in range(8):
            send_far[blocks[i], :] = (part(2, i) + recv[1, blocks[i], :].astype(F32)).astype(BF)
        far = remote(send_far, recv_far, sems.at[2, 0], sems.at[2, 1], across)
        two.wait_recv()
        far.wait_recv()
        for i in range(8):
            put(i, part(0, i) + recv[0, blocks[i], :].astype(F32) + recv_far[blocks[i], :].astype(F32))
        return one, two, far

    def grads_part(m, i):
        block = order[seq_of(xh ^ (m >> 1), (y + 4 - i // 2) % 4, c ^ (m & 1)) * 2 + i % 2]
        return jnp.concatenate([dkw[block], dvw[block]], axis=1)

    def put_grads(i, value):
        gg[i * 64 : i * 64 + 64, :] = value.astype(BF)

    sent = list(summed(grads_part, put_grads, sa, ra, sx, rx, xsem))
    back = []
    for d in (1, 2, 3):
        back.append(remote(gg.at[pl.ds(d * 128, 128)], kvg.at[d], ssem.at[8, d], rsem.at[8, d], along[4 - d]))
    own_g = pltpu.make_async_copy(gg.at[pl.ds(0, 128)], kvg.at[0], lsem.at[1])
    own_g.start()
    for d in (1, 3, 2):
        feats[d].wait_recv()
    for m in (3, 1, 2, 0):
        at = (xh ^ (m >> 1)) * 2 + (c ^ (m & 1))
        rows = pl.ds(pl.multiple_of(at * 512, 512), 512)
        acc[m] = jnp.dot(ht[rows, :], gg[...], preferred_element_type=F32)

    def put_rows(i, value):
        sf[2 * i] = value[0:32, :].astype(BF)
        sf[2 * i + 1] = value[32:64, :].astype(BF)

    sent += summed(lambda m, i: acc[m, i * 64 : i * 64 + 64, :], put_rows, sb, rb, sy, ry, ysem)

    def batch_copy(t):
        to = (b + t) % 16
        return remote_copy(sf.at[to], rf.at[t], fsend.at[t], frecv.at[t], (to, s))

    @pl.loop(1, 16)
    def _(t):
        batch_copy(t).start()

    rf[0] = sf[b]

    @pl.loop(1, 16)
    def _(t):
        batch_copy(t).wait_recv()

    total = jnp.sum(rf[...].astype(F32), axis=0)
    for t in range(4):
        wsum[t] = total[t * 8 : t * 8 + 8, :]
    tail = [remote(wsum.at[(y + d) % 4], wout.at[d], ssem.at[9, d], rsem.at[9, d], along[d]) for d in (1, 2, 3)]
    own_w = pltpu.make_async_copy(wsum.at[y], wout.at[0], lsem.at[2])
    own_w.start()

    @pl.loop(1, 16)
    def _(t):
        batch_copy(t).wait_send()

    for copy in (own_q, own_g, own_w):
        copy.wait()
    for d in (1, 2, 3):
        home_copy(d).wait()
        feats[d].wait_send()
        for copy in rows_in[d]:
            copy.wait_send()
    for copy in (*kv, far, side, *sent):
        copy.wait_send()
    last.wait_send()
    for copy in (*back, *tail):
        copy.wait()


def finish_kernel(dqh, kvg, wout, dq, dk, dv, kw, vw):
    _, _, _, y, _ = place()
    dq[...] = dqh[...]
    for d in range(4):
        head = lanes((y + d) % 4, 128)
        dk[:, head] = kvg[d, :, 0:128]
        dv[:, head] = kvg[d, :, 128:256]
        head = lanes((y + 4 - d) % 4, 128)
        kw[:, head] = wout[d, :, 0:128]
        vw[:, head] = wout[d, :, 128:256]


VMEM = pl.BlockSpec(memory_space=pltpu.VMEM)
SMEM = pl.BlockSpec(memory_space=pltpu.SMEM)
ANY = pl.BlockSpec(memory_space=pl.ANY)


def struct(shape, dtype):
    return jax.ShapeDtypeStruct(shape, dtype)


def shards(hidden_in, queries, key_states, value_states, grad_out, log_sums, deltas, block_order):
    DMA = pltpu.SemaphoreType.DMA
    dqh, kvg, wout = pl.pallas_call(
        fused_kernel,
        out_shape=(struct((128, 2048), BF), struct((4, 128, 256), BF), struct((4, 8, 256), F32)),
        in_specs=[SMEM] + [ANY] * 7,
        out_specs=(ANY,) * 3,
        scratch_shapes=[
            pltpu.VMEM((128, 2048), BF),
            pltpu.VMEM((4, 128, 512), BF),
            pltpu.VMEM((4, 128, 512), BF),
            pltpu.VMEM((32, 64, 256), BF),
            pltpu.VMEM((4, 4, 128), F32),
            pltpu.VMEM((4, 4, 128), F32),
            pltpu.VMEM((2048, 128), BF),
            pltpu.VMEM((2048, 512), BF),
            pltpu.VMEM((8, 256, 128), BF),
            pltpu.VMEM((8, 256, 128), BF),
            pltpu.VMEM((8, 128, 256), BF),
            pltpu.VMEM((2, 256, 128), BF),
            pltpu.VMEM((2, 256, 128), BF),
            pltpu.VMEM((2, 1, 256), F32),
            pltpu.VMEM((2, 1, 256), F32),
            pltpu.VMEM((1024, 128), F32),
            pltpu.VMEM((1024, 128), F32),
            pltpu.VMEM((32, 64, 128), F32),
            pltpu.VMEM((32, 64, 128), F32),
            pltpu.VMEM((20, 256, 128), F32),
            pltpu.VMEM((20, 256, 128), F32),
            pltpu.VMEM((2, 128, 256), F32),
            pltpu.VMEM((4, 128, 512), BF),
            pltpu.VMEM((2, 512, 256), BF),
            pltpu.VMEM((2, 512, 256), BF),
            pltpu.VMEM((512, 256), BF),
            pltpu.VMEM((512, 256), BF),
            pltpu.VMEM((512, 256), BF),
            pltpu.VMEM((4, 512, 256), F32),
            pltpu.VMEM((2, 512, 256), BF),
            pltpu.VMEM((2, 512, 256), BF),
            pltpu.VMEM((512, 256), BF),
            pltpu.VMEM((512, 256), BF),
            pltpu.VMEM((16, 32, 256), BF),
            pltpu.VMEM((16, 32, 256), BF),
            pltpu.VMEM((4, 8, 256), F32),
            DMA((10, 4)),
            DMA((10, 4)),
            DMA((3, 2)),
            DMA((3, 2)),
            DMA((16,)),
            DMA((16,)),
            DMA((7,)),
        ],
        name="fused",
        compiler_params=pltpu.CompilerParams(collective_id=0, has_side_effects=True),
    )(
        block_order,
        queries[0],
        grad_out[0],
        key_states.reshape(2, 64, 512),
        value_states.reshape(2, 64, 512),
        log_sums.reshape(4, 4, 128),
        deltas.reshape(4, 4, 128),
        hidden_in[0],
    )
    dq, dk, dv, kw, vw = pl.pallas_call(
        finish_kernel,
        out_shape=(
            struct((128, 2048), BF),
            struct((128, 512), BF),
            struct((128, 512), BF),
            struct((8, 512), F32),
            struct((8, 512), F32),
        ),
        in_specs=[VMEM] * 3,
        out_specs=(VMEM,) * 5,
        name="finish",
    )(dqh, kvg, wout)
    return (dq[None], dk[None], dv[None], kw, vw)


def solution(mesh):
    tokens, rows = P("batch", "seq", None), P("batch", None, "seq")
    return jax.shard_map(
        shards,
        mesh=mesh,
        in_specs=(tokens, tokens, tokens, tokens, tokens, rows, rows, P()),
        out_specs=(tokens, tokens, tokens, P(("batch", "seq"), None), P(("batch", "seq"), None)),
        check_vma=False,
    )
```

time: 491 us -> 75.4 us (0.15)
  waiting for transfers between devices: 269 us -> 0 us
  Pallas kernels: 0 us -> 73.9 us
  local copies, waits for them, and re-layouts: 69.4 us -> 0 us
  other arithmetic: 67.2 us -> 0 us
  matrix products: 55.4 us -> 0 us
  between operations: 14.2 us -> 0.64 us
  starting transfers between devices: 9.9 us -> 0 us
    ppermute x62 -> x0, waiting for transfers between devices: 157 us -> none  [passed_along(): return lax.ppermute(value, axis, pairs)]
    reduce_scatter x1 -> x0, waiting for transfers between devices: 101 us -> none  [shards(): lax.psum_scatter(jnp.einsum('td,te->de', flat_hidden, token_grads, prefer...]
    pallas_call x0 -> x2, Pallas kernels: none -> 73.9 us  [the longest x1 71.8 us: shards(): pl.pallas_call(fused_kernel, out_shape=(struct((128, 2048), BF), struct((...]
    dot_general x81 -> x0, matrix products: 55.4 us -> none  [the longest x32 32.8 us: head_scores(): jnp.einsum('bqhgd,bkhd->bhgqk', left_heads, right_heads, preferred_elemen...]
    add x48 -> x0, other arithmetic: 52.6 us -> none  [the longest x32 52.4 us: block_grads(): return (key_acc + key_part, value_acc + value_part, query_acc + query_part)]
    while x33 -> x0, local copies, waits for them, and re-layouts: 40.3 us -> none
    another operation x33 -> x0, local copies, waits for them, and re-layouts: 16.7 us -> none
    reduce_sum x17 -> x0, other arithmetic: 13 us -> none  [the longest x16 11.9 us: stored_positions(): block_ids = jnp.sum(jnp.where(matches, block_order[None, :], 0), axis=1)]
  transfers between devices with their start and end apart: 64 -> 0, of which waited for: 34 -> 0; matrix products, arithmetic and copies ran while one was open for 31% -> 0% of each run, Pallas kernels for 0% -> 0%
where the time goes in v2:
time: 75.4 us; the launch traced here: 74.5 us
  Pallas kernels  73.9 us (98%)
    pallas_call x1, Pallas kernels, shards(): pl.pallas_call(fused_kernel, out_shape=(struct((128, 2048), BF), struct((...  71.8 us
    pallas_call x1, Pallas kernels, shards(): pl.pallas_call(finish_kernel, out_shape=(struct((128, 2048), BF), struct(...  2.08 us

profile of v2, /device:TPU:2, one launch (start us, length us, event | category | flops | bytes accessed | tf_op | source)
XLA Modules:
  0.0 74.5 jit_solution(18366699961895677405)
XLA Ops:
  0.6 71.8 %fused.1 = (bf16[128,2048]{1,0:T(8,128)(2,1)}, bf16[4,128,256]{2,1,0:T(8,128)(2,1)}, f32[4,8,256]{2,1,0:T(8,128)}) custom-call(s32[32]{0:T(128)} %order.1, bf16[128,2048]{1,0:T(8,128)(2,1)} %bitcast.10, bf16[128,2048]{1,0:T(8,128)(2,1)} %bitcast.11, bf16[2,64,512]{2,1,0:T(8,128)(2,1)} %bitcast.13, bf16[2,64,512]{2,1,0:T(8,128)(2,1)} %bitcast.14, ...), custom_call_target="tpu_custom_call" | custom-call | tf_op jit(solution)/shard_map/fused/pallas_call | solution.py:350
  72.5 2.1 %finish.1 = (bf16[128,2048]{1,0:T(8,128)(2,1)}, bf16[128,512]{1,0:T(8,128)(2,1)}, bf16[128,512]{1,0:T(8,128)(2,1)}, f32[8,512]{1,0:T(8,128)}, f32[8,512]{1,0:T(8,128)}) custom-call(bf16[128,2048]{1,0:T(8,128)(2,1)} %get-tuple-element.13.dqh, bf16[4,128,256]{2,1,0:T(8,128)(2,1)} %get-tuple-element.14.kvg, f32[4,8,256]{2,1,0:T(8,128)} %get-tuple-element.15.wout), custom_call_target="tpu_custom_call" | custom-call | tf_op jit(solution)/shard_map/finish/pallas_call | solution.py:412

commit v3 on v2

--- a/solution.py
+++ b/solution.py
@@ -42,8 +42,8 @@
 
 
 def fused_kernel(
-    order, q, do, k, v, lse, dl, hid_in, dqh, kvg, wout,
-    hid, qx, dox, kvx, lx, dx, hts, ht, ks, vs, kt, qs, dos, lsv, dlv, dka, dva, dkw, dvw, ek, ev, dqt, dqx,
+    order, q, do, k_in, v_in, lse, dl, hid_in, dqh, kvg, wout,
+    hid, k, v, qx, dox, kvx, lx, dx, ht, ks, vs, kt, qs, dos, lsv, dlv, dka, dva, dkw, dvw, ek, ev, dqt, dqx,
     sa, ra, sx, rx, gg, acc, sb, rb, sy, ry, sf, rf, wsum,
     ssem, rsem, xsem, ysem, fsend, frecv, lsem,
 ):
@@ -51,9 +51,13 @@
     along = [None] + [(b, seq_of(xh, (y + d) % 4, c)) for d in (1, 2, 3)]
     partner, across = (b, seq_of(xh, y, 1 - c)), (b, seq_of(1 - xh, y, c))
 
+    keys_in = pltpu.make_async_copy(k_in, k, lsem.at[7])
+    values_in = pltpu.make_async_copy(v_in, v, lsem.at[8])
+    keys_in.start()
+    values_in.start()
     own = [
-        pltpu.make_async_copy(k.at[:, :, lanes(y, 128)], kvx.at[pl.ds(0, 2), :, pl.ds(0, 128)], lsem.at[0]),
-        pltpu.make_async_copy(v.at[:, :, lanes(y, 128)], kvx.at[pl.ds(0, 2), :, pl.ds(128, 128)], lsem.at[1]),
+        pltpu.make_async_copy(k_in.at[:, :, lanes(y, 128)], kvx.at[pl.ds(0, 2), :, pl.ds(0, 128)], lsem.at[0]),
+        pltpu.make_async_copy(v_in.at[:, :, lanes(y, 128)], kvx.at[pl.ds(0, 2), :, pl.ds(128, 128)], lsem.at[1]),
         pltpu.make_async_copy(q.at[:, lanes(y, 512)], qx.at[0], lsem.at[2]),
         pltpu.make_async_copy(do.at[:, lanes(y, 512)], dox.at[0], lsem.at[3]),
         pltpu.make_async_copy(lse.at[y], lx.at[0], lsem.at[4]),
@@ -74,11 +78,13 @@
 
     pl.semaphore_wait(barrier, 20)
 
-    kv = []
-    for d in (2, 1, 3):
-        t, to = (y + d) % 4, pl.ds(2 * d, 2)
-        kv.append(remote(k.at[:, :, lanes(t, 128)], kvx.at[to, :, pl.ds(0, 128)], ssem.at[0, d], rsem.at[0, d], along[d]))
-        kv.append(remote(v.at[:, :, lanes(t, 128)], kvx.at[to, :, pl.ds(128, 128)], ssem.at[1, d], rsem.at[1, d], along[d]))
+    keys_in.wait()
+    values_in.wait()
+    kv = [[], []]
+    for part, (source, half) in enumerate(((k, pl.ds(0, 128)), (v, pl.ds(128, 128)))):
+        for d in (2, 1, 3):
+            from_, to = source.at[:, :, lanes((y + d) % 4, 128)], kvx.at[pl.ds(2 * d, 2), :, half]
+            kv[part].append(remote(from_, to, ssem.at[part, d], rsem.at[part, d], along[d]))
     rows_in = {}
     for d in (1, 3, 2):
         t = (y + d) % 4
@@ -97,18 +103,22 @@
     for i in range(16):
         turned = lax.dot_general(pick, hid[:, i * 128 : i * 128 + 128], NT, preferred_element_type=F32).astype(BF)
         for p in range(4):
-            hts[p * 512 + i * 32 : p * 512 + i * 32 + 32, :] = turned[p * 32 : p * 32 + 32, :]
+            ht[0, p * 512 + i * 32 : p * 512 + i * 32 + 32, :] = turned[p * 32 : p * 32 + 32, :]
     feats = {}
-    for d in (1, 3, 2):
-        feats[d] = remote(hts, ht.at[:, pl.ds(d * 128, 128)], ssem.at[6, d], rsem.at[6, d], along[d])
-    ht[:, 0:128] = hts[...]
+    for d in (1, 3):
+        feats[d] = remote(ht.at[0], ht.at[d], ssem.at[6, d], rsem.at[6, d], along[d])
 
     for copy in own:
         copy.wait()
-    for copy in kv:
-        copy.wait_recv()
-    far = remote(kvx.at[pl.ds(0, 8)], kvx.at[pl.ds(16, 8)], ssem.at[0, 0], rsem.at[0, 0], across)
-    side = remote(kvx.at[pl.ds(0, 8)], kvx.at[pl.ds(8, 8)], ssem.at[1, 0], rsem.at[1, 0], partner)
+    far, side = [], []
+    for part in range(2):
+        for copy in kv[part]:
+            copy.wait_recv()
+        half = pl.ds(part * 128, 128)
+        mine, theirs = kvx.at[pl.ds(0, 8), :, half], kvx.at[pl.ds(16, 8), :, half]
+        far.append(remote(mine, theirs, ssem.at[part, 0], rsem.at[part, 0], across))
+        theirs = kvx.at[pl.ds(8, 8), :, half]
+        side.append(remote(mine, theirs, ssem.at[2 + part, 0], rsem.at[2 + part, 0], partner))
     slot_of = [None] * 32
     firsts = [order[2 * i] for i in range(16)]
     for n in range(16):
@@ -118,16 +128,20 @@
         pair, flip = code // 2, code % 2
         index = (((pair // 8) ^ xh) * 2 + ((pair % 2) ^ c)) * 8 + ((y + 4 - (pair // 2) % 4) % 4) * 2
         slot_of[n], slot_of[31 - n] = index + flip, index + 1 - flip
-    far.wait_recv()
-    last = remote(kvx.at[pl.ds(16, 8)], kvx.at[pl.ds(24, 8)], ssem.at[2, 0], rsem.at[2, 0], partner)
     gap = (
         lax.broadcasted_iota(jnp.int32, (256, 256), 0)
         - lax.broadcasted_iota(jnp.int32, (256, 256), 1) % 64
     )
     dka[0:1024, :] = jnp.zeros((1024, 128), F32)
     dva[0:1024, :] = jnp.zeros((1024, 128), F32)
-    side.wait_recv()
-    last.wait_recv()
+    last = []
+    for part in range(2):
+        far[part].wait_recv()
+        half = pl.ds(part * 128, 128)
+        mine, theirs = kvx.at[pl.ds(16, 8), :, half], kvx.at[pl.ds(24, 8), :, half]
+        last.append(remote(mine, theirs, ssem.at[4 + part, 0], rsem.at[4 + part, 0], partner))
+    for copy in (*side, *last):
+        copy.wait_recv()
     for n in range(32):
         both = kvx[slot_of[n]]
         ks[n // 4, n % 4 * 64 : n % 4 * 64 + 64, :] = both[:, 0:128]
@@ -218,10 +232,6 @@
             dqx[d, 0:64, h * 128 : h * 128 + 128] = jnp.where(flip, hi, lo)
             dqx[d, 64:128, h * 128 : h * 128 + 128] = jnp.where(flip, lo, hi)
 
-        @pl.when(turn > 0)
-        def _():
-            home_copy(d).start()
-
     own_q = pltpu.make_async_copy(dqx.at[0], dqh.at[:, lanes(y, 512)], lsem.at[0])
     own_q.start()
     quads = [low_of(d) // 4 for d in range(4)]
@@ -241,23 +251,30 @@
                         total += jnp.where(7 - n == quads[d], extra[d * 5 + 4, sub, :], 0.0)
                 whole[n * 4 + part] = total
 
-    def summed(part, put, send, recv, send_far, recv_far, sems):
+    def summed(part, put, after, send, recv, send_far, recv_far, sems):
         blocks = [slice(i * 64, i * 64 + 64) for i in range(8)]
-        for i in range(8):
-            send[1, blocks[i], :] = part(3, i).astype(BF)
-        one = remote(send.at[1], recv.at[1], sems.at[0, 0], sems.at[0, 1], partner)
-        for i in range(8):
-            send[0, blocks[i], :] = part(1, i).astype(BF)
-        two = remote(send.at[0], recv.at[0], sems.at[1, 0], sems.at[1, 1], partner)
-        one.wait_recv()
-        for i in range(8):
-            send_far[blocks[i], :] = (part(2, i) + recv[1, blocks[i], :].astype(F32)).astype(BF)
-        far = remote(send_far, recv_far, sems.at[2, 0], sems.at[2, 1], across)
-        two.wait_recv()
-        far.wait_recv()
-        for i in range(8):
-            put(i, part(0, i) + recv[0, blocks[i], :].astype(F32) + recv_far[blocks[i], :].astype(F32))
-        return one, two, far
+        chunks = [(n, pl.ds(n * 256, 256), range(n * 4, n * 4 + 4)) for n in range(2)]
+        one, two, far = [], [], []
+        for n, rows, members in chunks:
+            for i in members:
+                send[1, blocks[i], :] = part(3, i).astype(BF)
+            one.append(remote(send.at[1, rows], recv.at[1, rows], sems.at[0, 0, n], sems.at[0, 1, n], partner))
+        for n, rows, members in chunks:
+            for i in members:
+                send[0, blocks[i], :] = part(1, i).astype(BF)
+            two.append(remote(send.at[0, rows], recv.at[0, rows], sems.at[1, 0, n], sems.at[1, 1, n], partner))
+        for n, rows, members in chunks:
+            one[n].wait_recv()
+            for i in members:
+                send_far[blocks[i], :] = (part(2, i) + recv[1, blocks[i], :].astype(F32)).astype(BF)
+            far.append(remote(send_far.at[rows], recv_far.at[rows], sems.at[2, 0, n], sems.at[2, 1, n], across))
+        for n, rows, members in chunks:
+            two[n].wait_recv()
+            far[n].wait_recv()
+            for i in members:
+                put(i, part(0, i) + recv[0, blocks[i], :].astype(F32) + recv_far[blocks[i], :].astype(F32))
+            after(n)
+        return one + two + far
 
     def grads_part(m, i):
         block = order[seq_of(xh ^ (m >> 1), (y + 4 - i // 2) % 4, c ^ (m & 1)) * 2 + i % 2]
@@ -266,33 +283,44 @@
     def put_grads(i, value):
         gg[i * 64 : i * 64 + 64, :] = value.astype(BF)
 
-    sent = list(summed(grads_part, put_grads, sa, ra, sx, rx, xsem))
+    relays = []
+    for d, to, half in ((1, 1, 0), (3, 3, 1)):
+        feats[d].wait_recv()
+        rows = pl.ds(half * 1024, 1024)
+        relays.append(remote(ht.at[d, rows], ht.at[2, rows], ssem.at[6, 2 * half], rsem.at[6, 2 * half], along[to]))
+    sent = summed(grads_part, put_grads, lambda n: None, sa, ra, sx, rx, xsem)
     back = []
     for d in (1, 2, 3):
         back.append(remote(gg.at[pl.ds(d * 128, 128)], kvg.at[d], ssem.at[8, d], rsem.at[8, d], along[4 - d]))
     own_g = pltpu.make_async_copy(gg.at[pl.ds(0, 128)], kvg.at[0], lsem.at[1])
     own_g.start()
+    for copy in relays:
+        copy.wait_recv()
     for d in (1, 3, 2):
-        feats[d].wait_recv()
+        home_copy(d).start()
     for m in (3, 1, 2, 0):
         at = (xh ^ (m >> 1)) * 2 + (c ^ (m & 1))
         rows = pl.ds(pl.multiple_of(at * 512, 512), 512)
-        acc[m] = jnp.dot(ht[rows, :], gg[...], preferred_element_type=F32)
+        acc[m] = jnp.dot(
+            jnp.concatenate([ht[d, rows, :] for d in range(4)], axis=1), gg[...], preferred_element_type=F32
+        )
 
     def put_rows(i, value):
         sf[2 * i] = value[0:32, :].astype(BF)
         sf[2 * i + 1] = value[32:64, :].astype(BF)
 
-    sent += summed(lambda m, i: acc[m, i * 64 : i * 64 + 64, :], put_rows, sb, rb, sy, ry, ysem)
-
     def batch_copy(t):
         to = (b + t) % 16
         return remote_copy(sf.at[to], rf.at[t], fsend.at[t], frecv.at[t], (to, s))
 
-    @pl.loop(1, 16)
-    def _(t):
-        batch_copy(t).start()
-
+    def spread(n):
+        @pl.loop(n * 8, n * 8 + 8)
+        def _(to):
+            @pl.when(to != b)
+            def _():
+                batch_copy((to + 16 - b) % 16).start()
+
+    sent += summed(lambda m, i: acc[m, i * 64 : i * 64 + 64, :], put_rows, spread, sb, rb, sy, ry, ysem)
     rf[0] = sf[b]
 
     @pl.loop(1, 16)
@@ -314,12 +342,10 @@
         copy.wait()
     for d in (1, 2, 3):
         home_copy(d).wait()
-        feats[d].wait_send()
         for copy in rows_in[d]:
             copy.wait_send()
-    for copy in (*kv, far, side, *sent):
+    for copy in (feats[1], feats[3], *relays, *kv[0], *kv[1], *far, *side, *last, *sent):
         copy.wait_send()
-    last.wait_send()
     for copy in (*back, *tail):
         copy.wait()
 
@@ -354,13 +380,14 @@
         out_specs=(ANY,) * 3,
         scratch_shapes=[
             pltpu.VMEM((128, 2048), BF),
+            pltpu.VMEM((2, 64, 512), BF),
+            pltpu.VMEM((2, 64, 512), BF),
             pltpu.VMEM((4, 128, 512), BF),
             pltpu.VMEM((4, 128, 512), BF),
             pltpu.VMEM((32, 64, 256), BF),
             pltpu.VMEM((4, 4, 128), F32),
             pltpu.VMEM((4, 4, 128), F32),
-            pltpu.VMEM((2048, 128), BF),
-            pltpu.VMEM((2048, 512), BF),
+            pltpu.VMEM((4, 2048, 128), BF),
             pltpu.VMEM((8, 256, 128), BF),
             pltpu.VMEM((8, 256, 128), BF),
             pltpu.VMEM((8, 128, 256), BF),
@@ -391,11 +418,11 @@
             pltpu.VMEM((4, 8, 256), F32),
             DMA((10, 4)),
             DMA((10, 4)),
-            DMA((3, 2)),
-            DMA((3, 2)),
+            DMA((3, 2, 2)),
+            DMA((3, 2, 2)),
             DMA((16,)),
             DMA((16,)),
-            DMA((7,)),
+            DMA((9,)),
         ],
         name="fused",
         compiler_params=pltpu.CompilerParams(collective_id=0, has_side_effects=True),

time: 75.4 us -> 69.8 us (0.926)
  Pallas kernels: 73.9 us -> 68.1 us
    pallas_call x1, Pallas kernels: 71.8 us -> 66 us  [shards(): pl.pallas_call(fused_kernel, out_shape=(struct((128, 2048), BF), struct((...]
where the time goes in v3:
time: 69.8 us; the launch traced here: 68.8 us
  Pallas kernels  68.1 us (98%)
    pallas_call x1, Pallas kernels, shards(): pl.pallas_call(fused_kernel, out_shape=(struct((128, 2048), BF), struct((...  66 us
    pallas_call x1, Pallas kernels, shards(): pl.pallas_call(finish_kernel, out_shape=(struct((128, 2048), BF), struct(...  2.08 us

profile of v3, /device:TPU:2, one launch (start us, length us, event | category | flops | bytes accessed | tf_op | source)
XLA Modules:
  0.0 68.8 jit_solution(6343946361852297166)
XLA Ops:
  0.6 66.0 %fused.1 = (bf16[128,2048]{1,0:T(8,128)(2,1)}, bf16[4,128,256]{2,1,0:T(8,128)(2,1)}, f32[4,8,256]{2,1,0:T(8,128)}) custom-call(s32[32]{0:T(128)} %order.1, bf16[128,2048]{1,0:T(8,128)(2,1)} %bitcast.10, bf16[128,2048]{1,0:T(8,128)(2,1)} %bitcast.11, bf16[2,64,512]{2,1,0:T(8,128)(2,1)} %bitcast.13, bf16[2,64,512]{2,1,0:T(8,128)(2,1)} %bitcast.14, ...), custom_call_target="tpu_custom_call" | custom-call | tf_op jit(solution)/shard_map/fused/pallas_call | solution.py:376
  66.7 2.1 %finish.1 = (bf16[128,2048]{1,0:T(8,128)(2,1)}, bf16[128,512]{1,0:T(8,128)(2,1)}, bf16[128,512]{1,0:T(8,128)(2,1)}, f32[8,512]{1,0:T(8,128)}, f32[8,512]{1,0:T(8,128)}) custom-call(bf16[128,2048]{1,0:T(8,128)(2,1)} %get-tuple-element.13.dqh, bf16[4,128,256]{2,1,0:T(8,128)(2,1)} %get-tuple-element.14.kvg, f32[4,8,256]{2,1,0:T(8,128)} %get-tuple-element.15.wout), custom_call_target="tpu_custom_call" | custom-call | tf_op jit(solution)/shard_map/finish/pallas_call | solution.py:439

commit v4 on v3

--- a/solution.py
+++ b/solution.py
@@ -156,12 +156,15 @@
         first = first_of(d)
         return jnp.minimum(first, 31 - first)
 
-    def piece(h, n, block):
+    def products(h, n, block):
         scores = lax.dot_general(ks[n], qs[h], NT, preferred_element_type=F32)
+        dprobs = lax.dot_general(vs[n], dos[h], NT, preferred_element_type=F32)
+        return h, n, block, scores, dprobs
+
+    def parts(h, n, block, scores, dprobs):
         probs = jnp.exp2(scores * (SCALE * LOG2E) - lsv[h])
         if block is not None:
             probs = jnp.where(gap <= block * 64 - n * 256, probs, 0.0)
-        dprobs = lax.dot_general(vs[n], dos[h], NT, preferred_element_type=F32)
         dscores = (probs * (dprobs - dlv[h]) * SCALE).astype(BF)
         return (
             jnp.dot(dscores, qs[h], preferred_element_type=F32),
@@ -208,24 +211,31 @@
             target[0] = jnp.where(flip, pairs[1], pairs[0])
             target[1] = jnp.where(flip, pairs[0], pairs[1])
         dqt[...] = jnp.zeros_like(dqt)
-        for n in range(4):
-            dk, dv, dq = piece(1, n, None)
-            dka[n * 256 : n * 256 + 256, :] += dk
-            dva[n * 256 : n * 256 + 256, :] += dv
-            dqt[1] += dq
-        for j in range(4):
-            is_low = j <= quad
-            dk, dv, dq = piece(
-                jnp.where(is_low, 0, 1), jnp.where(is_low, j, 7 - j), jnp.where(is_low, low, 31 - low)
-            )
-            ek[d * 5 + j] = dk
-            ev[d * 5 + j] = dv
-            dqt[0] += jnp.where(is_low, dq, 0.0)
-            dqt[1] += jnp.where(is_low, 0.0, dq)
-        dk, dv, dq = piece(1, 7 - quad, 31 - low)
-        ek[d * 5 + 4] = dk
-        ev[d * 5 + 4] = dv
-        dqt[1] += dq
+        lows = [j <= quad for j in range(4)]
+        todo = [(1, n, None) for n in range(4)]
+        todo += [
+            (jnp.where(lows[j], 0, 1), jnp.where(lows[j], j, 7 - j), jnp.where(lows[j], low, 31 - low))
+            for j in range(4)
+        ]
+        todo.append((1, 7 - quad, 31 - low))
+        ahead = products(*todo[0])
+        for i in range(9):
+            now = ahead
+            if i < 8:
+                ahead = products(*todo[i + 1])
+            dk, dv, dq = parts(*now)
+            if i < 4:
+                dka[i * 256 : i * 256 + 256, :] += dk
+                dva[i * 256 : i * 256 + 256, :] += dv
+                dqt[1] += dq
+                continue
+            ek[d * 5 + i - 4] = dk
+            ev[d * 5 + i - 4] = dv
+            if i < 8:
+                dqt[0] += jnp.where(lows[i - 4], dq, 0.0)
+                dqt[1] += jnp.where(lows[i - 4], 0.0, dq)
+            else:
+                dqt[1] += dq
         low_q, high_q = dqt[0].T, dqt[1].T
         for h in range(4):
             lo, hi = low_q[h * 64 : h * 64 + 64, :].astype(BF), high_q[h * 64 : h * 64 + 64, :].astype(BF)
@@ -251,7 +261,7 @@
                         total += jnp.where(7 - n == quads[d], extra[d * 5 + 4, sub, :], 0.0)
                 whole[n * 4 + part] = total
 
-    def summed(part, put, after, send, recv, send_far, recv_far, sems):
+    def summed(part, put, between, after, send, recv, send_far, recv_far, sems):
         blocks = [slice(i * 64, i * 64 + 64) for i in range(8)]
         chunks = [(n, pl.ds(n * 256, 256), range(n * 4, n * 4 + 4)) for n in range(2)]
         one, two, far = [], [], []
@@ -260,14 +270,15 @@
                 send[1, blocks[i], :] = part(3, i).astype(BF)
             one.append(remote(send.at[1, rows], recv.at[1, rows], sems.at[0, 0, n], sems.at[0, 1, n], partner))
         for n, rows, members in chunks:
-            for i in members:
-                send[0, blocks[i], :] = part(1, i).astype(BF)
-            two.append(remote(send.at[0, rows], recv.at[0, rows], sems.at[1, 0, n], sems.at[1, 1, n], partner))
-        for n, rows, members in chunks:
             one[n].wait_recv()
             for i in members:
                 send_far[blocks[i], :] = (part(2, i) + recv[1, blocks[i], :].astype(F32)).astype(BF)
             far.append(remote(send_far.at[rows], recv_far.at[rows], sems.at[2, 0, n], sems.at[2, 1, n], across))
+        between()
+        for n, rows, members in chunks:
+            for i in members:
+                send[0, blocks[i], :] = part(1, i).astype(BF)
+            two.append(remote(send.at[0, rows], recv.at[0, rows], sems.at[1, 0, n], sems.at[1, 1, n], partner))
         for n, rows, members in chunks:
             two[n].wait_recv()
             far[n].wait_recv()
@@ -284,26 +295,42 @@
         gg[i * 64 : i * 64 + 64, :] = value.astype(BF)
 
     relays = []
-    for d, to, half in ((1, 1, 0), (3, 3, 1)):
-        feats[d].wait_recv()
-        rows = pl.ds(half * 1024, 1024)
-        relays.append(remote(ht.at[d, rows], ht.at[2, rows], ssem.at[6, 2 * half], rsem.at[6, 2 * half], along[to]))
-    sent = summed(grads_part, put_grads, lambda n: None, sa, ra, sx, rx, xsem)
+
+    def relay():
+        for d in (1, 3):
+            feats[d].wait_recv()
+        for late in range(2):
+            for d in (1, 3):
+                at = ((1 - xh) if late == 0 else xh) * 2 + d // 2
+                rows = pl.ds(pl.multiple_of(at * 512, 512), 512)
+                sems = (ssem.at[9 + 2 * late, d], rsem.at[9 + 2 * late, d])
+                relays.append(remote(ht.at[d, rows], ht.at[2, rows], *sems, along[d]))
+
+    sent = summed(grads_part, put_grads, relay, lambda n: None, sa, ra, sx, rx, xsem)
     back = []
     for d in (1, 2, 3):
         back.append(remote(gg.at[pl.ds(d * 128, 128)], kvg.at[d], ssem.at[8, d], rsem.at[8, d], along[4 - d]))
     own_g = pltpu.make_async_copy(gg.at[pl.ds(0, 128)], kvg.at[0], lsem.at[1])
     own_g.start()
-    for copy in relays:
-        copy.wait_recv()
-    for d in (1, 3, 2):
-        home_copy(d).start()
-    for m in (3, 1, 2, 0):
+
+    def outer(m):
         at = (xh ^ (m >> 1)) * 2 + (c ^ (m & 1))
         rows = pl.ds(pl.multiple_of(at * 512, 512), 512)
-        acc[m] = jnp.dot(
-            jnp.concatenate([ht[d, rows, :] for d in range(4)], axis=1), gg[...], preferred_element_type=F32
-        )
+        features = jnp.concatenate([ht[d, rows, :] for d in range(4)], axis=1)
+        acc[m] = jnp.dot(features, gg[...], preferred_element_type=F32)
+
+    for copy in relays[:2]:
+        copy.wait_recv()
+    outer(3)
+    outer(2)
+
+    def rest():
+        for copy in relays[2:]:
+            copy.wait_recv()
+        outer(1)
+        outer(0)
+        for d in (1, 3, 2):
+            home_copy(d).start()
 
     def put_rows(i, value):
         sf[2 * i] = value[0:32, :].astype(BF)
@@ -320,7 +347,7 @@
             def _():
                 batch_copy((to + 16 - b) % 16).start()
 
-    sent += summed(lambda m, i: acc[m, i * 64 : i * 64 + 64, :], put_rows, spread, sb, rb, sy, ry, ysem)
+    sent += summed(lambda m, i: acc[m, i * 64 : i * 64 + 64, :], put_rows, rest, spread, sb, rb, sy, ry, ysem)
     rf[0] = sf[b]
 
     @pl.loop(1, 16)
@@ -330,7 +357,7 @@
     total = jnp.sum(rf[...].astype(F32), axis=0)
     for t in range(4):
         wsum[t] = total[t * 8 : t * 8 + 8, :]
-    tail = [remote(wsum.at[(y + d) % 4], wout.at[d], ssem.at[9, d], rsem.at[9, d], along[d]) for d in (1, 2, 3)]
+    tail = [remote(wsum.at[(y + d) % 4], wout.at[d], ssem.at[10, d], rsem.at[10, d], along[d]) for d in (1, 2, 3)]
     own_w = pltpu.make_async_copy(wsum.at[y], wout.at[0], lsem.at[2])
     own_w.start()
 
@@ -416,8 +443,8 @@
             pltpu.VMEM((16, 32, 256), BF),
             pltpu.VMEM((16, 32, 256), BF),
             pltpu.VMEM((4, 8, 256), F32),
-            DMA((10, 4)),
-            DMA((10, 4)),
+            DMA((12, 4)),
+            DMA((12, 4)),
             DMA((3, 2, 2)),
             DMA((3, 2, 2)),
             DMA((16,)),

time: 69.8 us -> 66.1 us (0.947); the launches traced: 68.8 us -> 66 us
  Pallas kernels: 68.1 us -> 65.3 us
    pallas_call x1, Pallas kernels: 66 us -> 63.2 us  [shards(): pl.pallas_call(fused_kernel, out_shape=(struct((128, 2048), BF), struct((...]
where the time goes in v4:
time: 66.1 us; the launch traced here: 66 us
  Pallas kernels  65.3 us (99%)
    pallas_call x1, Pallas kernels, shards(): pl.pallas_call(fused_kernel, out_shape=(struct((128, 2048), BF), struct((...  63.2 us
    pallas_call x1, Pallas kernels, shards(): pl.pallas_call(finish_kernel, out_shape=(struct((128, 2048), BF), struct(...  2.08 us

profile of v4, /device:TPU:2, one launch (start us, length us, event | category | flops | bytes accessed | tf_op | source)
XLA Modules:
  0.0 66.0 jit_solution(3268923379311355265)
XLA Ops:
  0.6 63.2 %fused.1 = (bf16[128,2048]{1,0:T(8,128)(2,1)}, bf16[4,128,256]{2,1,0:T(8,128)(2,1)}, f32[4,8,256]{2,1,0:T(8,128)}) custom-call(s32[32]{0:T(128)} %order.1, bf16[128,2048]{1,0:T(8,128)(2,1)} %bitcast.10, bf16[128,2048]{1,0:T(8,128)(2,1)} %bitcast.11, bf16[2,64,512]{2,1,0:T(8,128)(2,1)} %bitcast.13, bf16[2,64,512]{2,1,0:T(8,128)(2,1)} %bitcast.14, ...), custom_call_target="tpu_custom_call" | custom-call | tf_op jit(solution)/shard_map/fused/pallas_call | solution.py:403
  63.9 2.1 %finish.1 = (bf16[128,2048]{1,0:T(8,128)(2,1)}, bf16[128,512]{1,0:T(8,128)(2,1)}, bf16[128,512]{1,0:T(8,128)(2,1)}, f32[8,512]{1,0:T(8,128)}, f32[8,512]{1,0:T(8,128)}) custom-call(bf16[128,2048]{1,0:T(8,128)(2,1)} %get-tuple-element.13.dqh, bf16[4,128,256]{2,1,0:T(8,128)(2,1)} %get-tuple-element.14.kvg, f32[4,8,256]{2,1,0:T(8,128)} %get-tuple-element.15.wout), custom_call_target="tpu_custom_call" | custom-call | tf_op jit(solution)/shard_map/finish/pallas_call | solution.py:466

commit v5 on v4

--- a/solution.py
+++ b/solution.py
@@ -105,8 +105,11 @@
         for p in range(4):
             ht[0, p * 512 + i * 32 : p * 512 + i * 32 + 32, :] = turned[p * 32 : p * 32 + 32, :]
     feats = {}
-    for d in (1, 3):
-        feats[d] = remote(ht.at[0], ht.at[d], ssem.at[6, d], rsem.at[6, d], along[d])
+    for late in range(2):
+        rows = pl.ds(pl.multiple_of((xh if late else 1 - xh) * 1024, 1024), 1024)
+        for d in (1, 3):
+            sems = (ssem.at[6 + 6 * late, d], rsem.at[6 + 6 * late, d])
+            feats[d, late] = remote(ht.at[0, rows], ht.at[d, rows], *sems, along[d])
 
     for copy in own:
         copy.wait()
@@ -261,7 +264,7 @@
                         total += jnp.where(7 - n == quads[d], extra[d * 5 + 4, sub, :], 0.0)
                 whole[n * 4 + part] = total
 
-    def summed(part, put, between, after, send, recv, send_far, recv_far, sems):
+    def summed(part, put, between, behind, after, send, recv, send_far, recv_far, sems):
         blocks = [slice(i * 64, i * 64 + 64) for i in range(8)]
         chunks = [(n, pl.ds(n * 256, 256), range(n * 4, n * 4 + 4)) for n in range(2)]
         one, two, far = [], [], []
@@ -279,6 +282,7 @@
             for i in members:
                 send[0, blocks[i], :] = part(1, i).astype(BF)
             two.append(remote(send.at[0, rows], recv.at[0, rows], sems.at[1, 0, n], sems.at[1, 1, n], partner))
+        behind()
         for n, rows, members in chunks:
             two[n].wait_recv()
             far[n].wait_recv()
@@ -296,20 +300,15 @@
 
     relays = []
 
-    def relay():
+    def relay(late):
         for d in (1, 3):
-            feats[d].wait_recv()
-        for late in range(2):
-            for d in (1, 3):
-                at = ((1 - xh) if late == 0 else xh) * 2 + d // 2
-                rows = pl.ds(pl.multiple_of(at * 512, 512), 512)
-                sems = (ssem.at[9 + 2 * late, d], rsem.at[9 + 2 * late, d])
-                relays.append(remote(ht.at[d, rows], ht.at[2, rows], *sems, along[d]))
-
-    sent = summed(grads_part, put_grads, relay, lambda n: None, sa, ra, sx, rx, xsem)
+            feats[d, late].wait_recv()
+            rows = pl.ds(pl.multiple_of(((xh if late else 1 - xh) * 2 + d // 2) * 512, 512), 512)
+            sems = (ssem.at[9 + 2 * late, d], rsem.at[9 + 2 * late, d])
+            relays.append(remote(ht.at[d, rows], ht.at[2, rows], *sems, along[d]))
+
+    sent = summed(grads_part, put_grads, lambda: relay(0), lambda: relay(1), lambda n: None, sa, ra, sx, rx, xsem)
     back = []
-    for d in (1, 2, 3):
-        back.append(remote(gg.at[pl.ds(d * 128, 128)], kvg.at[d], ssem.at[8, d], rsem.at[8, d], along[4 - d]))
     own_g = pltpu.make_async_copy(gg.at[pl.ds(0, 128)], kvg.at[0], lsem.at[1])
     own_g.start()
 
@@ -331,6 +330,8 @@
         outer(0)
         for d in (1, 3, 2):
             home_copy(d).start()
+        for d in (1, 2, 3):
+            back.append(remote(gg.at[pl.ds(d * 128, 128)], kvg.at[d], ssem.at[8, d], rsem.at[8, d], along[4 - d]))
 
     def put_rows(i, value):
         sf[2 * i] = value[0:32, :].astype(BF)
@@ -347,7 +348,7 @@
             def _():
                 batch_copy((to + 16 - b) % 16).start()
 
-    sent += summed(lambda m, i: acc[m, i * 64 : i * 64 + 64, :], put_rows, rest, spread, sb, rb, sy, ry, ysem)
+    sent += summed(lambda m, i: acc[m, i * 64 : i * 64 + 64, :], put_rows, rest, lambda: None, spread, sb, rb, sy, ry, ysem)
     rf[0] = sf[b]
 
     @pl.loop(1, 16)
@@ -371,7 +372,7 @@
         home_copy(d).wait()
         for copy in rows_in[d]:
             copy.wait_send()
-    for copy in (feats[1], feats[3], *relays, *kv[0], *kv[1], *far, *side, *last, *sent):
+    for copy in (*feats.values(), *relays, *kv[0], *kv[1], *far, *side, *last, *sent):
         copy.wait_send()
     for copy in (*back, *tail):
         copy.wait()
@@ -443,8 +444,8 @@
             pltpu.VMEM((16, 32, 256), BF),
             pltpu.VMEM((16, 32, 256), BF),
             pltpu.VMEM((4, 8, 256), F32),
-            DMA((12, 4)),
-            DMA((12, 4)),
+            DMA((13, 4)),
+            DMA((13, 4)),
             DMA((3, 2, 2)),
             DMA((3, 2, 2)),
             DMA((16,)),

time: 66.1 us -> 64.2 us (0.971)
  Pallas kernels: 65.3 us -> 63.5 us
    pallas_call x1, Pallas kernels: 63.2 us -> 61.4 us  [shards(): pl.pallas_call(fused_kernel, out_shape=(struct((128, 2048), BF), struct((...]
where the time goes in v5:
time: 64.2 us; the launch traced here: 64.1 us
  Pallas kernels  63.5 us (99%)
    pallas_call x1, Pallas kernels, shards(): pl.pallas_call(fused_kernel, out_shape=(struct((128, 2048), BF), struct((...  61.4 us
    pallas_call x1, Pallas kernels, shards(): pl.pallas_call(finish_kernel, out_shape=(struct((128, 2048), BF), struct(...  2.08 us

profile of v5, /device:TPU:2, one launch (start us, length us, event | category | flops | bytes accessed | tf_op | source)
XLA Modules:
  0.0 64.1 jit_solution(9924842580266209250)
XLA Ops:
  0.6 61.4 %fused.1 = (bf16[128,2048]{1,0:T(8,128)(2,1)}, bf16[4,128,256]{2,1,0:T(8,128)(2,1)}, f32[4,8,256]{2,1,0:T(8,128)}) custom-call(s32[32]{0:T(128)} %order.1, bf16[128,2048]{1,0:T(8,128)(2,1)} %bitcast.10, bf16[128,2048]{1,0:T(8,128)(2,1)} %bitcast.11, bf16[2,64,512]{2,1,0:T(8,128)(2,1)} %bitcast.13, bf16[2,64,512]{2,1,0:T(8,128)(2,1)} %bitcast.14, ...), custom_call_target="tpu_custom_call" | custom-call | tf_op jit(solution)/shard_map/fused/pallas_call | solution.py:404
  62.0 2.1 %finish.1 = (bf16[128,2048]{1,0:T(8,128)(2,1)}, bf16[128,512]{1,0:T(8,128)(2,1)}, bf16[128,512]{1,0:T(8,128)(2,1)}, f32[8,512]{1,0:T(8,128)}, f32[8,512]{1,0:T(8,128)}) custom-call(bf16[128,2048]{1,0:T(8,128)(2,1)} %get-tuple-element.13.dqh, bf16[4,128,256]{2,1,0:T(8,128)(2,1)} %get-tuple-element.14.kvg, f32[4,8,256]{2,1,0:T(8,128)} %get-tuple-element.15.wout), custom_call_target="tpu_custom_call" | custom-call | tf_op jit(solution)/shard_map/finish/pallas_call | solution.py:467
